TPU v7x, 128 devices: a whole 4x4x4 slice. The times are simulated.
128 devices in a mesh: frame: 8 (over x, core), seq: 16 (over y, z).
Axes of the slice: x: 4, y: 4, z: 4, core: 2. Of those that a mesh axis runs over, the one named last changes fastest.
Arguments:
- vit_states: bfloat16 [256, 256, 1280], P(('frame', 'seq')), may hold values from -6 to 6
- frame_slot: int32 [128], replicated, may hold values from 0 to 255, as said below
- patch_count: int32 [128], replicated, may hold values from 208 to 256, as said below
- vis_start: int32 [128], replicated, may hold values from 0 to 16383, as said below
- text_embed: bfloat16 [128, 128, 4096], P(None, ('frame', 'seq')), may hold values from -6 to 6
- vit_ln_gain: float32 [1280], replicated, may hold values from 0.25 to 1.75
- vit_ln_bias: float32 [1280], replicated, may hold values from -1.5 to 1.5
- vit_qkv_w: bfloat16 [1280, 3840], P('seq'), may hold values from -0.15625 to 0.15625
- vit_qkv_b: float32 [3840], replicated, may hold values from -1.5 to 1.5
- vit_out_w: bfloat16 [1280, 1280], P('seq'), may hold values from -0.15625 to 0.15625
- vit_out_b: float32 [1280], replicated, may hold values from -1.5 to 1.5
- proj_w: bfloat16 [1280, 4096], replicated, may hold values from -0.15625 to 0.15625
- proj_b: float32 [4096], replicated, may hold values from -1.5 to 1.5
- attn_gain: float32 [4096], replicated, may hold values from 0.25 to 1.75
- wq: bfloat16 [4096, 2048], P(None, 'frame'), may hold values from -0.09375 to 0.09375
- wk: bfloat16 [4096, 1024], P(None, 'frame'), may hold values from -0.09375 to 0.09375
- wv: bfloat16 [4096, 1024], P(None, 'frame'), may hold values from -0.09375 to 0.09375
- wo: bfloat16 [2048, 4096], P('frame'), may hold values from -0.125 to 0.125
Outputs:
- mixed: bfloat16 [128, 128, 4096], P(None, ('frame', 'seq'))
Inputs may be any that keep to these rules, and one draw needn't show every extreme that they name: Frame t sits in slot frame_slot[t]; slot k of the device with index d (axes frame then seq) is d * 2 + k; no slot holds two frames. The two devices with frame indices 2i and 2i+1 and the same seq index hold exactly two frames between them; some device holds 2 frames. `patch_count`: A multiple of 4; some frame has 256 patches. Frame t's patch_count[t] / 4 visual positions start at vis_start[t] and lie within positions t * 128 to (t + 1) * 128 - 1.
All inputs are finite; a program needn't handle non-finite values.
Results may differ from a plain program's by a relative error of at most 0.015.
Values may be sent and summed in bfloat16 or wider, within the bound.
A program may use at most 128 MiB of HBM per device.

v0:
```python
import math

import jax
import jax.numpy as jnp
from jax import lax
from jax.sharding import PartitionSpec as P

VHEADS = 16
HEAD_WIDTH = 128


rope_theta = 500000.0
vit_epsilon = 1e-06
norm_epsilon = 1e-05
masked_score = -1e30


def partner_2(value, axis, stride):
    mask = 2**stride
    pairs = [(source, source ^ mask) for source in range(lax.axis_size(axis))]
    return lax.ppermute(value, axis, pairs)


def in_one_piece(arrays, axis, dim, along):
    widths = [a.shape[along] for a in arrays]
    both = jnp.concatenate(arrays, axis=along)
    result = lax.all_gather(both, axis, axis=dim, tiled=True)
    return tuple(jnp.split(result, [sum(widths[:k]) for k in range(1, len(widths))], axis=along))


def apply_rotary(values, rotary_angles):
    half_width = values.shape[-1] // 2
    first_half = values[..., :half_width]
    second_half = values[..., half_width:]
    cosine = jnp.cos(rotary_angles)
    sine_part = jnp.sin(rotary_angles)
    return jnp.concatenate(
        [
            first_half * cosine - second_half * sine_part,
            second_half * cosine + first_half * sine_part,
        ],
        axis=-1,
    )


def rope_angles(positions, head_size):
    exponents = jnp.arange(0, head_size, 2).astype(jnp.float32) / head_size
    inverse = jnp.power(jnp.float32(rope_theta), -exponents)
    return positions.astype(jnp.float32)[:, None] * inverse[None, :]


def add_columns(left, shard_piece):
    return jnp.dot(left, shard_piece, preferred_element_type=jnp.float32)


def per_device(
    vit_states,
    frame_slot,
    patch_count,
    vis_start,
    text_embed,
    vit_ln_gain,
    vit_ln_bias,
    vit_qkv_w,
    vit_qkv_b,
    vit_out_w,
    vit_out_b,
    proj_w,
    proj_b,
    attn_gain,
    wq,
    wk,
    wv,
    wo,
):
    frames_n = lax.axis_size("frame")
    seqs_n = lax.axis_size("seq")
    devices_n = frames_n * seqs_n
    my_frame = lax.axis_index("frame")
    my_seq = lax.axis_index("seq")
    my_device = my_frame * seqs_n + my_seq
    slots_held = vit_states.shape[0]
    frame_max = vit_states.shape[1]
    width_vit = vit_states.shape[2]
    vis_max = frame_max // 4
    own_rows = text_embed.shape[0]
    laps = (vis_max + devices_n - 1) // devices_n
    frame_ids = jnp.arange(frame_slot.shape[0])
    holder = frame_slot // slots_held
    holder_frame = holder // seqs_n
    pair_low = (holder_frame - holder_frame % 2) * seqs_n + holder % seqs_n
    pair_order = holder_frame % 2 * slots_held + frame_slot % slots_held
    same_pair = pair_low[:, None] == pair_low[None, :]
    earlier = pair_order[None, :] < pair_order[:, None]
    pair_rank = jnp.sum((same_pair & earlier).astype(jnp.int32), axis=1)
    partner = partner_2(vit_states, "frame", 0)
    low_side = my_frame % 2 == 0
    four_slots = jnp.where(
        low_side,
        jnp.concatenate([vit_states, partner], 0),
        jnp.concatenate([partner, vit_states], 0),
    )
    my_low = (my_frame - my_frame % 2) * seqs_n + my_seq
    picked = (pair_low == my_low) & (pair_rank == my_frame % 2)
    my_frame_id = jnp.sum(jnp.where(picked, frame_ids, 0))
    my_order = jnp.sum(jnp.where(picked, pair_order, 0))
    states = lax.dynamic_slice_in_dim(four_slots, my_order, 1, 0)
    slots_n = 1
    slot_frames = jnp.reshape(my_frame_id, (1,))
    slot_live = jnp.ones((1,), jnp.bool_)
    source_device = pair_low + pair_rank * seqs_n
    slot_count = jnp.where(slot_live, patch_count[slot_frames], frame_max)
    slot_start = vis_start[slot_frames]
    patch_rows = states.reshape(slots_n * frame_max, width_vit)
    rows_wide = patch_rows.astype(jnp.float32)
    average = jnp.mean(rows_wide, axis=1, keepdims=True)
    centred = rows_wide - average
    spread = jnp.mean(centred * centred, axis=1, keepdims=True)
    normed_states = (centred * lax.rsqrt(spread + vit_epsilon) * vit_ln_gain + vit_ln_bias).astype(
        jnp.bfloat16
    )
    projected_vit = add_columns(normed_states, lax.all_gather(vit_qkv_w, "seq", axis=0, tiled=True))
    projected_vit = (projected_vit + vit_qkv_b).astype(jnp.bfloat16)
    head_size = width_vit // VHEADS
    shaped = projected_vit.reshape(slots_n, frame_max, 3, VHEADS, head_size)
    scores = jnp.einsum(
        "sqhd,skhd->shqk", shaped[:, :, 0], shaped[:, :, 1], preferred_element_type=jnp.float32
    ) / math.sqrt(head_size)
    key_live = jnp.arange(frame_max)[None, :] < slot_count[:, None]
    scores = jnp.where(key_live[:, None, None, :], scores, masked_score)
    highest = jnp.max(scores, axis=-1, keepdims=True)
    weights = jnp.exp(scores - highest)
    probabilities = (weights / jnp.sum(weights, axis=-1, keepdims=True)).astype(jnp.bfloat16)
    context_vit = jnp.einsum(
        "shqk,skhd->sqhd", probabilities, shaped[:, :, 2], preferred_element_type=jnp.float32
    ).astype(jnp.bfloat16)
    context_vit = context_vit.reshape(patch_rows.shape[0], width_vit)
    attended = add_columns(context_vit, lax.all_gather(vit_out_w, "seq", axis=0, tiled=True))
    hidden = (rows_wide + attended + vit_out_b).astype(jnp.bfloat16)
    pooled = jnp.mean(
        hidden.astype(jnp.float32).reshape(slots_n, vis_max, 4, width_vit), axis=2
    ).astype(jnp.bfloat16)
    owners = jnp.arange(devices_n)
    lap_ids = jnp.arange(laps)
    distance = jnp.mod(owners[:, None] - slot_start[None, :], devices_n)
    token_ids = distance[:, :, None] + lap_ids[None, None, :] * devices_n
    sent_live = (token_ids < (slot_count // 4)[None, :, None]) & slot_live[None, :, None]
    token_clip = jnp.minimum(token_ids, vis_max - 1)
    slot_ids = jnp.arange(slots_n)[None, :, None]
    outgoing = jnp.where(
        sent_live[..., None], pooled[slot_ids, token_clip], jnp.zeros((), jnp.bfloat16)
    )
    arrived = lax.all_to_all(outgoing, ("frame", "seq"), split_axis=0, concat_axis=0, tiled=True)
    local_ids = jnp.arange(own_rows)
    positions = local_ids * devices_n + my_device
    token_frame = positions // own_rows
    within = positions - vis_start[token_frame]
    is_visual = (within >= 0) & (within < patch_count[token_frame] // 4)
    within_clip = jnp.clip(within, 0, vis_max - 1)
    flat_index = source_device[token_frame] * slots_n * laps + within_clip // devices_n
    table = arrived.reshape(devices_n * slots_n * laps, arrived.shape[-1])
    fetched = table[flat_index]
    fetched = (jnp.dot(fetched, proj_w, preferred_element_type=jnp.float32) + proj_b).astype(
        jnp.bfloat16
    )
    text_rows = text_embed.reshape(own_rows, text_embed.shape[-1])
    merged = jnp.where(is_visual[:, None], fetched, text_rows)
    merged_wide = merged.astype(jnp.float32)
    normed_tok = (
        merged_wide
        * lax.rsqrt(jnp.mean(merged_wide * merged_wide, axis=1, keepdims=True) + norm_epsilon)
        * attn_gain
    ).astype(jnp.bfloat16)
    shard_piece = lax.all_gather(normed_tok, "frame", axis=0, tiled=True)
    projected = jnp.concatenate(
        [
            jnp.dot(shard_piece, wq, preferred_element_type=jnp.float32),
            jnp.dot(shard_piece, wk, preferred_element_type=jnp.float32),
            jnp.dot(shard_piece, wv, preferred_element_type=jnp.float32),
        ],
        axis=1,
    )
    query_width = wq.shape[1]
    kv_width = wk.shape[1]
    group_rows = projected.shape[0]
    kv_heads = kv_width // HEAD_WIDTH
    query_heads = query_width // HEAD_WIDTH
    row_ids = jnp.arange(group_rows)
    group_positions = row_ids % own_rows * devices_n + row_ids // own_rows * seqs_n + my_seq
    rotary_angles = rope_angles(group_positions, HEAD_WIDTH)[:, None, :]
    query_matrix = apply_rotary(
        projected[:, :query_width].reshape(group_rows, query_heads, HEAD_WIDTH), rotary_angles
    ).astype(jnp.bfloat16)
    keys_own = apply_rotary(
        projected[:, query_width : query_width + kv_width].reshape(
            group_rows, kv_heads, HEAD_WIDTH
        ),
        rotary_angles,
    ).astype(jnp.bfloat16)
    values_own = (
        projected[:, query_width + kv_width :]
        .astype(jnp.bfloat16)
        .reshape(group_rows, kv_heads, HEAD_WIDTH)
    )
    grouped_rows = query_matrix.reshape(group_rows, kv_heads, query_heads // kv_heads, HEAD_WIDTH)
    group_size = query_heads // kv_heads
    start_state = (
        jnp.full((kv_heads, group_size, group_rows), masked_score, jnp.float32),
        jnp.zeros((kv_heads, group_size, group_rows), jnp.float32),
        jnp.zeros((kv_heads, group_size, group_rows, HEAD_WIDTH), jnp.float32),
    )
    carry = start_state
    key_piece, value_piece = in_one_piece((keys_own, values_own), "seq", 0, 1)
    piece_rows = key_piece.shape[0]
    inner_rows = math.gcd(piece_rows, 1024)
    steps_n = piece_rows // inner_rows
    key_blocks = key_piece.reshape(steps_n, inner_rows, kv_heads, HEAD_WIDTH)
    value_blocks = value_piece.reshape(steps_n, inner_rows, kv_heads, HEAD_WIDTH)
    block_offsets = inner_rows * jnp.arange(steps_n)

    def visit(running, operands):
        running_max, denominator, weighted = running
        key_block, value_block, block_offset = operands
        gathered_ids = block_offset + jnp.arange(inner_rows)
        seq_of = gathered_ids // group_rows
        inner_ids = gathered_ids % group_rows
        key_positions = inner_ids % own_rows * devices_n + inner_ids // own_rows * seqs_n + seq_of
        block_scores = jnp.einsum(
            "qkgd,nkd->kgqn", grouped_rows, key_block, preferred_element_type=jnp.float32
        ) / math.sqrt(HEAD_WIDTH)
        allowed = key_positions[None, :] <= group_positions[:, None]
        block_scores = jnp.where(allowed[None, None], block_scores, masked_score)
        new_max = jnp.maximum(running_max, jnp.max(block_scores, axis=-1))
        expd = jnp.where(allowed[None, None], jnp.exp(block_scores - new_max[..., None]), 0.0)
        rescale = jnp.exp(running_max - new_max)
        denominator = denominator * rescale + jnp.sum(expd, axis=-1)
        weighted = weighted * rescale[..., None] + jnp.einsum(
            "kgqn,nkd->kgqd",
            expd.astype(jnp.bfloat16),
            value_block,
            preferred_element_type=jnp.float32,
        )
        return ((new_max, denominator, weighted), None)

    carry, unused = lax.scan(visit, carry, (key_blocks, value_blocks, block_offsets))
    final_max, denominator, weighted = carry
    context_tok = (weighted / denominator[..., None]).astype(jnp.bfloat16)
    context_tok = jnp.transpose(context_tok, (2, 0, 1, 3)).reshape(group_rows, query_width)
    summed = lax.psum_scatter(
        jnp.dot(context_tok, wo, preferred_element_type=jnp.float32).astype(jnp.bfloat16),
        "frame",
        scatter_dimension=0,
        tiled=True,
    )
    return summed.reshape(own_rows, 1, wo.shape[1])


def solution(mesh):
    return jax.shard_map(
        per_device,
        mesh=mesh,
        in_specs=(
            P(("frame", "seq"), None, None),
            P(),
            P(),
            P(),
            P(None, ("frame", "seq"), None),
            P(),
            P(),
            P("seq", None),
            P(),
            P("seq", None),
            P(),
            P(),
            P(),
            P(),
            P(None, "frame"),
            P(None, "frame"),
            P(None, "frame"),
            P("frame", None),
        ),
        out_specs=P(None, ("frame", "seq"), None),
        check_vma=False,
    )
```

profile of v0, /device:TPU:1, one launch (start us, length us, event | category | flops | bytes accessed | tf_op | source)
XLA Modules:
  0.0 679.3 jit_solution(15090803585346122329)
XLA Ops:
  29.6 60.5 %all-gather.5.cloned.1.call-done = bf16[1280,3840]{1,0:T(8,128)(2,1)} async-done(((bf16[80,3840]{1,0:T(8,128)(2,1)}), bf16[1280,3840]{1,0:T(8,128)(2,1)}) %all-gather.5.cloned.1.call-update) | async-done | bytes 9830416 | tf_op jit(solution)/shard_map/all_gather | solution.py:122
  90.1 7.9 %fusion.52 = bf16[256,3840]{1,0:T(8,128)(2,1)} fusion(bf16[1280,3840]{1,0:T(8,128)(2,1)} %all-gather.5.cloned.1.call-done, f32[3840]{0:T(1024)S(1)} %copy-done.7, bf16[1,256,1280]{2,1,0:T(8,128)(2,1)S(1)} %get-tuple-element.286, f32[1280]{0:T(1024)S(1)} %copy-done.8, f32[1280]{0:T(1024)S(1)} %copy-done.9, f32[256]{0:T(256)S(1)} %add_rsqrt_fusion, ...), kind=kOutput, calls=%fused_computation.79 | convolution fusion | flops 2520514560 | bytes 12479488 | tf_op jit(solution)/shard_map/dot_general | solution.py:53
  98.0 4.0 copy.59
  105.7 2.4 fusion.67
  108.2 31.7 %all-gather.7.cloned.1.call-done = bf16[1280,1280]{1,0:T(8,128)(2,1)} async-done(((bf16[80,1280]{1,0:T(8,128)(2,1)}), bf16[1280,1280]{1,0:T(8,128)(2,1)}) %all-gather.7.cloned.1.call-update) | async-done | bytes 3276816 | tf_op jit(solution)/shard_map/all_gather | solution.py:138
  139.9 4.2 fusion.59
  144.1 2.6 reshape.802
  152.9 7.4 %all-to-all-start = ((bf16[128,2,640]{2,1,0:T(2,128)(2,1)}), bf16[128,2,640]{2,1,0:T(2,128)(2,1)S(1)}, u32[]{:S(2)}, u32[]{:S(2)}) async-start(bf16[128,2,640]{2,1,0:T(2,128)(2,1)} %reshape.851), calls=%async_computation | async-start | bytes 655360 | tf_op jit(solution)/shard_map/all_to_all | solution.py:153
  160.6 11.6 %all-to-all-done = bf16[128,2,640]{2,1,0:T(2,128)(2,1)S(1)} async-done(((bf16[128,2,640]{2,1,0:T(2,128)(2,1)}), bf16[128,2,640]{2,1,0:T(2,128)(2,1)S(1)}, u32[]{:S(2)}, u32[]{:S(2)}) %all-to-all-start) | async-done | bytes 327712 | tf_op jit(solution)/shard_map/all_to_all | solution.py:153
  173.5 6.3 multiply_reduce_fusion
  181.1 46.0 %all-gather.9.cloned.1.call-done = bf16[1024,4096]{1,0:T(8,128)(2,1)} async-done(((bf16[128,4096]{1,0:T(8,128)(2,1)}), bf16[1024,4096]{1,0:T(8,128)(2,1)}) %all-gather.9.cloned.1.call-update) | async-done | bytes 8388624 | tf_op jit(solution)/shard_map/all_gather | solution.py:174
  227.1 6.4 convolution_bitcast_fusion
  234.8 2.9 fusion.72
  238.9 3.1 multiply_cosine_fusion
  241.9 6.3 fusion.121
  250.8 2.4 copy.75
  256.1 53.2 %all-gather.11.cloned.1.call-done = bf16[16384,2,128]{0,2,1:T(8,128)(2,1)} async-done(((bf16[1024,2,128]{0,2,1:T(8,128)(2,1)}), bf16[16384,2,128]{0,2,1:T(8,128)(2,1)}) %all-gather.11.cloned.1.call-update) | async-done | bytes 8388624 | tf_op jit(solution)/shard_map/all_gather | solution.py:27
  309.3 5.8 fusion.118
  315.1 6.4 copy.71
  321.5 6.4 copy.72
  327.9 285.7 %while.20 = (s32[]{:T(128)}, f32[1,2,1024]{2,1,0:T(2,128)S(1)}, f32[1,2,1024]{2,1,0:T(2,128)S(1)}, f32[1,2,1024,128]{3,2,1,0:T(8,128)}, s32[16]{0:T(128)S(1)}, /...) while((s32[]{:T(128)}, f32[1,2,1024]{2,1,0:T(2,128)S(1)}, ...), condition=%wide.region_12.13_spmd.clone, body=%wide.region_9.12_spmd.clone.sunk | while | flops 1102912512 | bytes 66208936 | solution.py:245
  329.8 6.2 fusion.145
  336.0 7.2 %fusion.148 = f32[1,2,1024,128]{3,2,1,0:T(8,128)} fusion(f32[1024,1024,2]{1,0,2:T(8,128)} %get-tuple-element.376, f32[2,1024]{1,0:T(2,128)S(1)} %bitcast.180, pred[1024,1024]{0,1:T(8,128)(4,1)S(1)} %broadcast_compare_fusion.2, f32[1,2,1024,128]{3,2,1,0:T(8,128)} %get-tuple-element.392, f32[2,1024]{1,0:T(2,128)S(1)} %get-tuple-element.377, ...), kind=kOutput, calls=%fused_computation.16.clone.1 | convolution fusion | flops 548143104 | bytes 11813377 | tf_op jit(solution)/shard_map/while/body/eval_jaxpr/kgqn,nkd->kgqd/dot_general | solution.py:237
  343.2 2.2 fusion.147
  347.3 6.2 fusion.145
  353.5 7.5 %fusion.148 = f32[1,2,1024,128]{3,2,1,0:T(8,128)} fusion(f32[1024,1024,2]{1,0,2:T(8,128)} %get-tuple-element.376, f32[2,1024]{1,0:T(2,128)S(1)} %bitcast.180, pred[1024,1024]{0,1:T(8,128)(4,1)S(1)} %broadcast_compare_fusion.2, f32[1,2,1024,128]{3,2,1,0:T(8,128)} %get-tuple-element.392, f32[2,1024]{1,0:T(2,128)S(1)} %get-tuple-element.377, ...), kind=kOutput, calls=%fused_computation.16.clone.1 | convolution fusion | flops 548143104 | bytes 11813377 | tf_op jit(solution)/shard_map/while/body/eval_jaxpr/kgqn,nkd->kgqd/dot_general | solution.py:237
  361.1 2.2 fusion.147
  365.2 6.2 fusion.145
  371.4 7.5 %fusion.148 = f32[1,2,1024,128]{3,2,1,0:T(8,128)} fusion(f32[1024,1024,2]{1,0,2:T(8,128)} %get-tuple-element.376, f32[2,1024]{1,0:T(2,128)S(1)} %bitcast.180, pred[1024,1024]{0,1:T(8,128)(4,1)S(1)} %broadcast_compare_fusion.2, f32[1,2,1024,128]{3,2,1,0:T(8,128)} %get-tuple-element.392, f32[2,1024]{1,0:T(2,128)S(1)} %get-tuple-element.377, ...), kind=kOutput, calls=%fused_computation.16.clone.1 | convolution fusion | flops 548143104 | bytes 11813377 | tf_op jit(solution)/shard_map/while/body/eval_jaxpr/kgqn,nkd->kgqd/dot_general | solution.py:237
  378.9 2.2 fusion.147
  383.0 6.2 fusion.145
  389.2 7.5 %fusion.148 = f32[1,2,1024,128]{3,2,1,0:T(8,128)} fusion(f32[1024,1024,2]{1,0,2:T(8,128)} %get-tuple-element.376, f32[2,1024]{1,0:T(2,128)S(1)} %bitcast.180, pred[1024,1024]{0,1:T(8,128)(4,1)S(1)} %broadcast_compare_fusion.2, f32[1,2,1024,128]{3,2,1,0:T(8,128)} %get-tuple-element.392, f32[2,1024]{1,0:T(2,128)S(1)} %get-tuple-element.377, ...), kind=kOutput, calls=%fused_computation.16.clone.1 | convolution fusion | flops 548143104 | bytes 11813377 | tf_op jit(solution)/shard_map/while/body/eval_jaxpr/kgqn,nkd->kgqd/dot_general | solution.py:237
  400.9 6.2 fusion.145
  407.1 7.5 %fusion.148 = f32[1,2,1024,128]{3,2,1,0:T(8,128)} fusion(f32[1024,1024,2]{1,0,2:T(8,128)} %get-tuple-element.376, f32[2,1024]{1,0:T(2,128)S(1)} %bitcast.180, pred[1024,1024]{0,1:T(8,128)(4,1)S(1)} %broadcast_compare_fusion.2, f32[1,2,1024,128]{3,2,1,0:T(8,128)} %get-tuple-element.392, f32[2,1024]{1,0:T(2,128)S(1)} %get-tuple-element.377, ...), kind=kOutput, calls=%fused_computation.16.clone.1 | convolution fusion | flops 548143104 | bytes 11813377 | tf_op jit(solution)/shard_map/while/body/eval_jaxpr/kgqn,nkd->kgqd/dot_general | solution.py:237
  414.7 2.2 fusion.147
  418.8 6.2 fusion.145
  425.0 7.5 %fusion.148 = f32[1,2,1024,128]{3,2,1,0:T(8,128)} fusion(f32[1024,1024,2]{1,0,2:T(8,128)} %get-tuple-element.376, f32[2,1024]{1,0:T(2,128)S(1)} %bitcast.180, pred[1024,1024]{0,1:T(8,128)(4,1)S(1)} %broadcast_compare_fusion.2, f32[1,2,1024,128]{3,2,1,0:T(8,128)} %get-tuple-element.392, f32[2,1024]{1,0:T(2,128)S(1)} %get-tuple-element.377, ...), kind=kOutput, calls=%fused_computation.16.clone.1 | convolution fusion | flops 548143104 | bytes 11813377 | tf_op jit(solution)/shard_map/while/body/eval_jaxpr/kgqn,nkd->kgqd/dot_general | solution.py:237
  432.5 2.2 fusion.147
  436.6 6.2 fusion.145
  442.8 7.5 %fusion.148 = f32[1,2,1024,128]{3,2,1,0:T(8,128)} fusion(f32[1024,1024,2]{1,0,2:T(8,128)} %get-tuple-element.376, f32[2,1024]{1,0:T(2,128)S(1)} %bitcast.180, pred[1024,1024]{0,1:T(8,128)(4,1)S(1)} %broadcast_compare_fusion.2, f32[1,2,1024,128]{3,2,1,0:T(8,128)} %get-tuple-element.392, f32[2,1024]{1,0:T(2,128)S(1)} %get-tuple-element.377, ...), kind=kOutput, calls=%fused_computation.16.clone.1 | convolution fusion | flops 548143104 | bytes 11813377 | tf_op jit(solution)/shard_map/while/body/eval_jaxpr/kgqn,nkd->kgqd/dot_general | solution.py:237
  454.5 6.2 fusion.145
  460.7 7.5 %fusion.148 = f32[1,2,1024,128]{3,2,1,0:T(8,128)} fusion(f32[1024,1024,2]{1,0,2:T(8,128)} %get-tuple-element.376, f32[2,1024]{1,0:T(2,128)S(1)} %bitcast.180, pred[1024,1024]{0,1:T(8,128)(4,1)S(1)} %broadcast_compare_fusion.2, f32[1,2,1024,128]{3,2,1,0:T(8,128)} %get-tuple-element.392, f32[2,1024]{1,0:T(2,128)S(1)} %get-tuple-element.377, ...), kind=kOutput, calls=%fused_computation.16.clone.1 | convolution fusion | flops 548143104 | bytes 11813377 | tf_op jit(solution)/shard_map/while/body/eval_jaxpr/kgqn,nkd->kgqd/dot_general | solution.py:237
  468.2 2.2 fusion.147
  472.4 6.2 fusion.145
  478.5 7.5 %fusion.148 = f32[1,2,1024,128]{3,2,1,0:T(8,128)} fusion(f32[1024,1024,2]{1,0,2:T(8,128)} %get-tuple-element.376, f32[2,1024]{1,0:T(2,128)S(1)} %bitcast.180, pred[1024,1024]{0,1:T(8,128)(4,1)S(1)} %broadcast_compare_fusion.2, f32[1,2,1024,128]{3,2,1,0:T(8,128)} %get-tuple-element.392, f32[2,1024]{1,0:T(2,128)S(1)} %get-tuple-element.377, ...), kind=kOutput, calls=%fused_computation.16.clone.1 | convolution fusion | flops 548143104 | bytes 11813377 | tf_op jit(solution)/shard_map/while/body/eval_jaxpr/kgqn,nkd->kgqd/dot_general | solution.py:237
  490.2 6.2 fusion.145
  496.4 7.5 %fusion.148 = f32[1,2,1024,128]{3,2,1,0:T(8,128)} fusion(f32[1024,1024,2]{1,0,2:T(8,128)} %get-tuple-element.376, f32[2,1024]{1,0:T(2,128)S(1)} %bitcast.180, pred[1024,1024]{0,1:T(8,128)(4,1)S(1)} %broadcast_compare_fusion.2, f32[1,2,1024,128]{3,2,1,0:T(8,128)} %get-tuple-element.392, f32[2,1024]{1,0:T(2,128)S(1)} %get-tuple-element.377, ...), kind=kOutput, calls=%fused_computation.16.clone.1 | convolution fusion | flops 548143104 | bytes 11813377 | tf_op jit(solution)/shard_map/while/body/eval_jaxpr/kgqn,nkd->kgqd/dot_general | solution.py:237
  508.1 6.2 fusion.145
  514.3 7.5 %fusion.148 = f32[1,2,1024,128]{3,2,1,0:T(8,128)} fusion(f32[1024,1024,2]{1,0,2:T(8,128)} %get-tuple-element.376, f32[2,1024]{1,0:T(2,128)S(1)} %bitcast.180, pred[1024,1024]{0,1:T(8,128)(4,1)S(1)} %broadcast_compare_fusion.2, f32[1,2,1024,128]{3,2,1,0:T(8,128)} %get-tuple-element.392, f32[2,1024]{1,0:T(2,128)S(1)} %get-tuple-element.377, ...), kind=kOutput, calls=%fused_computation.16.clone.1 | convolution fusion | flops 548143104 | bytes 11813377 | tf_op jit(solution)/shard_map/while/body/eval_jaxpr/kgqn,nkd->kgqd/dot_general | solution.py:237
  521.8 2.2 fusion.147
  525.9 6.2 fusion.145
  532.1 7.5 %fusion.148 = f32[1,2,1024,128]{3,2,1,0:T(8,128)} fusion(f32[1024,1024,2]{1,0,2:T(8,128)} %get-tuple-element.376, f32[2,1024]{1,0:T(2,128)S(1)} %bitcast.180, pred[1024,1024]{0,1:T(8,128)(4,1)S(1)} %broadcast_compare_fusion.2, f32[1,2,1024,128]{3,2,1,0:T(8,128)} %get-tuple-element.392, f32[2,1024]{1,0:T(2,128)S(1)} %get-tuple-element.377, ...), kind=kOutput, calls=%fused_computation.16.clone.1 | convolution fusion | flops 548143104 | bytes 11813377 | tf_op jit(solution)/shard_map/while/body/eval_jaxpr/kgqn,nkd->kgqd/dot_general | solution.py:237
  543.8 6.2 fusion.145
  550.0 7.5 %fusion.148 = f32[1,2,1024,128]{3,2,1,0:T(8,128)} fusion(f32[1024,1024,2]{1,0,2:T(8,128)} %get-tuple-element.376, f32[2,1024]{1,0:T(2,128)S(1)} %bitcast.180, pred[1024,1024]{0,1:T(8,128)(4,1)S(1)} %broadcast_compare_fusion.2, f32[1,2,1024,128]{3,2,1,0:T(8,128)} %get-tuple-element.392, f32[2,1024]{1,0:T(2,128)S(1)} %get-tuple-element.377, ...), kind=kOutput, calls=%fused_computation.16.clone.1 | convolution fusion | flops 548143104 | bytes 11813377 | tf_op jit(solution)/shard_map/while/body/eval_jaxpr/kgqn,nkd->kgqd/dot_general | solution.py:237
  561.7 6.2 fusion.145
  567.9 7.5 %fusion.148 = f32[1,2,1024,128]{3,2,1,0:T(8,128)} fusion(f32[1024,1024,2]{1,0,2:T(8,128)} %get-tuple-element.376, f32[2,1024]{1,0:T(2,128)S(1)} %bitcast.180, pred[1024,1024]{0,1:T(8,128)(4,1)S(1)} %broadcast_compare_fusion.2, f32[1,2,1024,128]{3,2,1,0:T(8,128)} %get-tuple-element.392, f32[2,1024]{1,0:T(2,128)S(1)} %get-tuple-element.377, ...), kind=kOutput, calls=%fused_computation.16.clone.1 | convolution fusion | flops 548143104 | bytes 11813377 | tf_op jit(solution)/shard_map/while/body/eval_jaxpr/kgqn,nkd->kgqd/dot_general | solution.py:237
  575.4 2.2 fusion.147
  579.5 6.2 fusion.145
  585.7 7.5 %fusion.148 = f32[1,2,1024,128]{3,2,1,0:T(8,128)} fusion(f32[1024,1024,2]{1,0,2:T(8,128)} %get-tuple-element.376, f32[2,1024]{1,0:T(2,128)S(1)} %bitcast.180, pred[1024,1024]{0,1:T(8,128)(4,1)S(1)} %broadcast_compare_fusion.2, f32[1,2,1024,128]{3,2,1,0:T(8,128)} %get-tuple-element.392, f32[2,1024]{1,0:T(2,128)S(1)} %get-tuple-element.377, ...), kind=kOutput, calls=%fused_computation.16.clone.1 | convolution fusion | flops 548143104 | bytes 11813377 | tf_op jit(solution)/shard_map/while/body/eval_jaxpr/kgqn,nkd->kgqd/dot_general | solution.py:237
  597.4 6.2 fusion.145
  603.6 7.5 %fusion.148 = f32[1,2,1024,128]{3,2,1,0:T(8,128)} fusion(f32[1024,1024,2]{1,0,2:T(8,128)} %get-tuple-element.376, f32[2,1024]{1,0:T(2,128)S(1)} %bitcast.180, pred[1024,1024]{0,1:T(8,128)(4,1)S(1)} %broadcast_compare_fusion.2, f32[1,2,1024,128]{3,2,1,0:T(8,128)} %get-tuple-element.392, f32[2,1024]{1,0:T(2,128)S(1)} %get-tuple-element.377, ...), kind=kOutput, calls=%fused_computation.16.clone.1 | convolution fusion | flops 548143104 | bytes 11813377 | tf_op jit(solution)/shard_map/while/body/eval_jaxpr/kgqn,nkd->kgqd/dot_general | solution.py:237
  611.1 2.2 fusion.147
  615.4 5.6 convolution_convert_fusion
  621.0 51.8 %reduce-scatter.2.cloned.1.call-done = bf16[128,4096]{1,0:T(8,128)(2,1)} async-done(((bf16[1024,4096]{1,0:T(8,128)(2,1)}), bf16[128,4096]{1,0:T(8,128)(2,1)}) %reduce-scatter.2.cloned.1.call-update) | async-done | bytes 1048592 | tf_op jit(solution)/shard_map/reduce_scatter | solution.py:249
  (219 shorter events, 83.9 us)
Async XLA Ops:
  6.5 608.8 %copy-start = (bf16[256,4096]{1,0:T(8,128)(2,1)S(1)}, bf16[256,4096]{1,0:T(8,128)(2,1)}, u32[]{:S(2)}) copy-start(bf16[256,4096]{1,0:T(8,128)(2,1)} %param.37) | copy-start | bytes 6291460
  6.5 83.5 %copy-start.9 = (f32[1280]{0:T(1024)S(1)}, f32[1280]{0:T(1024)}, u32[]{:S(2)}) copy-start(f32[1280]{0:T(1024)} %param.25) | copy-start | bytes 15364
  6.5 83.5 %copy-start.8 = (f32[1280]{0:T(1024)S(1)}, f32[1280]{0:T(1024)}, u32[]{:S(2)}) copy-start(f32[1280]{0:T(1024)} %param.26) | copy-start | bytes 15364
  6.5 83.5 %copy-start.7 = (f32[3840]{0:T(1024)S(1)}, f32[3840]{0:T(1024)}, u32[]{:S(2)}) copy-start(f32[3840]{0:T(1024)} %param.28) | copy-start | bytes 46084
  6.5 83.5 %all-gather.5.cloned.1.call-start = ((), (), s32[]{:S(2)}) async-start(), calls=%async_computation.2 | async-start | bytes 10444800 | tf_op jit(solution)/shard_map/all_gather | solution.py:122
  7.3 132.6 %all-gather.7.cloned.1.call-start = ((), (), s32[]{:S(2)}) async-start(), calls=%async_computation.3 | async-start | bytes 3481600 | tf_op jit(solution)/shard_map/all_gather | solution.py:138
  8.0 19.3 %collective-permute-start = (bf16[2,256,1280]{2,1,0:T(8,128)(2,1)}, bf16[2,256,1280]{2,1,0:T(8,128)(2,1)}, u32[]{:S(2)}, u32[]{:S(2)}) collective-permute-start(bf16[2,256,1280]{2,1,0:T(8,128)(2,1)} %param.20), channel_id=1, source_target_pairs={{0,16},{16,0},{32,48},{48,32},{64,80},{80,64},{96,112},{112,96},{1... | collective-permute-start | bytes 3932168 | tf_op jit(solution)/shard_map/ppermute | solution.py:21
  105.7 34.2 %copy-start.10 = (f32[1280]{0:T(1024)S(1)}, f32[1280]{0:T(1024)}, u32[]{:S(2)}) copy-start(f32[1280]{0:T(1024)} %param.30) | copy-start | bytes 15364
  150.6 22.8 %copy-start.5 = (f32[4096]{0:T(1024)S(1)}, f32[4096]{0:T(1024)}, u32[]{:S(2)}) copy-start(f32[4096]{0:T(1024)} %param.32) | copy-start | bytes 49156
  152.9 19.3 %all-to-all-start = ((bf16[128,2,640]{2,1,0:T(2,128)(2,1)}), bf16[128,2,640]{2,1,0:T(2,128)(2,1)S(1)}, u32[]{:S(2)}, u32[]{:S(2)}) async-start(bf16[128,2,640]{2,1,0:T(2,128)(2,1)} %reshape.851), calls=%async_computation | async-start | bytes 655360 | tf_op jit(solution)/shard_map/all_to_all | solution.py:153
  160.4 66.8 %all-gather.9.cloned.1.call-start = ((), (), s32[]{:S(2)}) async-start(), calls=%async_computation.4 | async-start | bytes 9437184 | tf_op jit(solution)/shard_map/all_gather | solution.py:174
  173.5 6.3 copy-start.6
  179.7 47.4 %copy-start.3 = (bf16[4096,128]{1,0:T(8,128)(2,1)S(1)}, bf16[4096,128]{1,0:T(8,128)(2,1)}, u32[]{:S(2)}) copy-start(bf16[4096,128]{1,0:T(8,128)(2,1)} %param.35) | copy-start | bytes 3145732
  181.0 128.2 %all-gather.11.cloned.1.call-start = ((), (), s32[]{:S(2)}) async-start(), calls=%async_computation.5 | async-start | bytes 8912896 | tf_op jit(solution)/shard_map/all_gather | solution.py:27
  227.1 7.6 %copy-start.2 = (bf16[1024,4096]{1,0:T(8,128)(2,1)S(1)}, bf16[1024,4096]{1,0:T(8,128)(2,1)}, u32[]{:S(2)}) copy-start(bf16[1024,4096]{1,0:T(8,128)(2,1)} %all-gather.9.cloned.1.call-done) | copy-start | bytes 25165828
  227.1 7.6 %copy-start.4 = (bf16[4096,128]{1,0:T(8,128)(2,1)S(1)}, bf16[4096,128]{1,0:T(8,128)(2,1)}, u32[]{:S(2)}) copy-start(bf16[4096,128]{1,0:T(8,128)(2,1)} %param.36) | copy-start | bytes 3145732
  238.6 434.2 %reduce-scatter.2.cloned.1.call-start = ((), (), s32[]{:S(2)}) async-start(), calls=%async_computation.6 | async-start | bytes 9437184 | tf_op jit(solution)/shard_map/reduce_scatter | solution.py:249
  336.0 7.3 %copy-start.1 = (f32[1024,1024,2]{1,0,2:T(8,128)S(1)}, f32[1024,1024,2]{1,0,2:T(8,128)}, u32[]{:S(2)}) copy-start(f32[1024,1024,2]{1,0,2:T(8,128)} %get-tuple-element.376) | copy-start | bytes 25165828 | tf_op jit(solution)/shard_map/while
  353.5 7.6 %copy-start.1 = (f32[1024,1024,2]{1,0,2:T(8,128)S(1)}, f32[1024,1024,2]{1,0,2:T(8,128)}, u32[]{:S(2)}) copy-start(f32[1024,1024,2]{1,0,2:T(8,128)} %get-tuple-element.376) | copy-start | bytes 25165828 | tf_op jit(solution)/shard_map/while
  371.4 7.6 %copy-start.1 = (f32[1024,1024,2]{1,0,2:T(8,128)S(1)}, f32[1024,1024,2]{1,0,2:T(8,128)}, u32[]{:S(2)}) copy-start(f32[1024,1024,2]{1,0,2:T(8,128)} %get-tuple-element.376) | copy-start | bytes 25165828 | tf_op jit(solution)/shard_map/while
  389.2 7.6 %copy-start.1 = (f32[1024,1024,2]{1,0,2:T(8,128)S(1)}, f32[1024,1024,2]{1,0,2:T(8,128)}, u32[]{:S(2)}) copy-start(f32[1024,1024,2]{1,0,2:T(8,128)} %get-tuple-element.376) | copy-start | bytes 25165828 | tf_op jit(solution)/shard_map/while
  407.1 7.6 %copy-start.1 = (f32[1024,1024,2]{1,0,2:T(8,128)S(1)}, f32[1024,1024,2]{1,0,2:T(8,128)}, u32[]{:S(2)}) copy-start(f32[1024,1024,2]{1,0,2:T(8,128)} %get-tuple-element.376) | copy-start | bytes 25165828 | tf_op jit(solution)/shard_map/while
  425.0 7.6 %copy-start.1 = (f32[1024,1024,2]{1,0,2:T(8,128)S(1)}, f32[1024,1024,2]{1,0,2:T(8,128)}, u32[]{:S(2)}) copy-start(f32[1024,1024,2]{1,0,2:T(8,128)} %get-tuple-element.376) | copy-start | bytes 25165828 | tf_op jit(solution)/shard_map/while
  442.8 7.6 %copy-start.1 = (f32[1024,1024,2]{1,0,2:T(8,128)S(1)}, f32[1024,1024,2]{1,0,2:T(8,128)}, u32[]{:S(2)}) copy-start(f32[1024,1024,2]{1,0,2:T(8,128)} %get-tuple-element.376) | copy-start | bytes 25165828 | tf_op jit(solution)/shard_map/while
  460.7 7.6 %copy-start.1 = (f32[1024,1024,2]{1,0,2:T(8,128)S(1)}, f32[1024,1024,2]{1,0,2:T(8,128)}, u32[]{:S(2)}) copy-start(f32[1024,1024,2]{1,0,2:T(8,128)} %get-tuple-element.376) | copy-start | bytes 25165828 | tf_op jit(solution)/shard_map/while
  478.5 7.6 %copy-start.1 = (f32[1024,1024,2]{1,0,2:T(8,128)S(1)}, f32[1024,1024,2]{1,0,2:T(8,128)}, u32[]{:S(2)}) copy-start(f32[1024,1024,2]{1,0,2:T(8,128)} %get-tuple-element.376) | copy-start | bytes 25165828 | tf_op jit(solution)/shard_map/while
  496.4 7.6 %copy-start.1 = (f32[1024,1024,2]{1,0,2:T(8,128)S(1)}, f32[1024,1024,2]{1,0,2:T(8,128)}, u32[]{:S(2)}) copy-start(f32[1024,1024,2]{1,0,2:T(8,128)} %get-tuple-element.376) | copy-start | bytes 25165828 | tf_op jit(solution)/shard_map/while
  514.3 7.6 %copy-start.1 = (f32[1024,1024,2]{1,0,2:T(8,128)S(1)}, f32[1024,1024,2]{1,0,2:T(8,128)}, u32[]{:S(2)}) copy-start(f32[1024,1024,2]{1,0,2:T(8,128)} %get-tuple-element.376) | copy-start | bytes 25165828 | tf_op jit(solution)/shard_map/while
  532.1 7.6 %copy-start.1 = (f32[1024,1024,2]{1,0,2:T(8,128)S(1)}, f32[1024,1024,2]{1,0,2:T(8,128)}, u32[]{:S(2)}) copy-start(f32[1024,1024,2]{1,0,2:T(8,128)} %get-tuple-element.376) | copy-start | bytes 25165828 | tf_op jit(solution)/shard_map/while
  550.0 7.6 %copy-start.1 = (f32[1024,1024,2]{1,0,2:T(8,128)S(1)}, f32[1024,1024,2]{1,0,2:T(8,128)}, u32[]{:S(2)}) copy-start(f32[1024,1024,2]{1,0,2:T(8,128)} %get-tuple-element.376) | copy-start | bytes 25165828 | tf_op jit(solution)/shard_map/while
  567.8 7.6 %copy-start.1 = (f32[1024,1024,2]{1,0,2:T(8,128)S(1)}, f32[1024,1024,2]{1,0,2:T(8,128)}, u32[]{:S(2)}) copy-start(f32[1024,1024,2]{1,0,2:T(8,128)} %get-tuple-element.376) | copy-start | bytes 25165828 | tf_op jit(solution)/shard_map/while
  585.7 7.6 %copy-start.1 = (f32[1024,1024,2]{1,0,2:T(8,128)S(1)}, f32[1024,1024,2]{1,0,2:T(8,128)}, u32[]{:S(2)}) copy-start(f32[1024,1024,2]{1,0,2:T(8,128)} %get-tuple-element.376) | copy-start | bytes 25165828 | tf_op jit(solution)/shard_map/while
  603.6 7.6 %copy-start.1 = (f32[1024,1024,2]{1,0,2:T(8,128)S(1)}, f32[1024,1024,2]{1,0,2:T(8,128)}, u32[]{:S(2)}) copy-start(f32[1024,1024,2]{1,0,2:T(8,128)} %get-tuple-element.376) | copy-start | bytes 25165828 | tf_op jit(solution)/shard_map/while
Sparse Core Ops, SparseCore 0:
  9.5 80.4 all-gather.4
  92.3 47.5 all-gather.6
  181.2 45.9 all-gather.8
  238.7 70.5 all-gather.10
  621.1 51.6 reduce-scatter.1
where the time goes:
time: 681 us; the launch traced here: 679 us
  matrix products  263 us (39%)
  waiting for transfers between devices  256 us (38%)
  other arithmetic  76.8 us (11%)
  local copies, waits for them, and re-layouts  52.4 us (8%)
  between operations  20.1 us (3%)
  starting transfers between devices  9.5 us (1%)
    dot_general x16, matrix products, visit(): jnp.einsum('kgqn,nkd->kgqd', expd.astype(jnp.bfloat16), value_block, pref...  120 us
    dot_general x16, matrix products, visit(): jnp.einsum('qkgd,nkd->kgqn', grouped_rows, key_block, preferred_element_t...  98.7 us
    all_gather x1, waiting for transfers between devices, per_device(): lax.all_gather(vit_qkv_w, 'seq', axis=0, tiled=True)  60.5 us
    all_gather x1, waiting for transfers between devices, in_one_piece(): result = lax.all_gather(both, axis, axis=dim, tiled=True)  53.2 us
    reduce_scatter x1, waiting for transfers between devices, per_device(): lax.psum_scatter(jnp.dot(context_tok, wo, preferred_element_type=jnp.floa...  51.8 us
    all_gather x1, waiting for transfers between devices, per_device(): shard_piece = lax.all_gather(normed_tok, 'frame', axis=0, tiled=True)  46 us
    reduce_sum x16, other arithmetic, visit(): denominator = denominator * rescale + jnp.sum(expd, axis=-1)  35.8 us
    all_gather x1, waiting for transfers between devices, per_device(): lax.all_gather(vit_out_w, 'seq', axis=0, tiled=True)  31.7 us
  transfers between devices with their start and end apart: 7, of which 6 were waited for; matrix products, arithmetic and copies ran while one was open for 7% of the time, Pallas kernels for 0%

commit v1 on v0

v1 whole, which is shorter than its diff:
```python
import functools
import math

import jax
import jax.numpy as jnp
from jax import lax
from jax.experimental import pallas as pl
from jax.experimental.pallas import tpu as pltpu
from jax.sharding import PartitionSpec as P

MESH = pl.DeviceIdType.MESH
BF = jnp.bfloat16
F32 = jnp.float32
NEG = -1e30
ROPE_THETA = 500000.0
NEAR_FIRST = (1, 3, 2)


def remote(src, dst, send, recv, f, s):
    return pltpu.make_async_remote_copy(
        src_ref=src,
        dst_ref=dst,
        send_sem=send,
        recv_sem=recv,
        device_id={"frame": f, "seq": s},
        device_id_type=MESH,
    )


def places():
    f = lax.axis_index("frame")
    s = lax.axis_index("seq")
    y, z = s // 4, s % 4

    def along_y(k):
        return (y + k) % 4 * 4 + z

    def along_z(k):
        return y * 4 + (z + k) % 4

    def along_x(k):
        return (f // 2 + k) % 4 * 2 + f % 2

    partner = f + 1 - 2 * (f % 2)
    return f, s, along_x, along_y, along_z, partner


def greet(peers):
    barrier = pltpu.get_barrier_semaphore()
    for f, s in peers:
        pl.semaphore_signal(
            barrier, inc=1, device_id={"frame": f, "seq": s}, device_id_type=MESH
        )
    pl.semaphore_wait(barrier, len(peers))


def gather_kernel(w, t, v, wg, tg, vg, local, wss, wrs, tss, trs, vss, vrs):
    f, s, xs, ys, zs, fp = places()
    greet(
        [(f, ys(k)) for k in (1, 2, 3)]
        + [(f, zs(k)) for k in (1, 2, 3)]
        + [(xs(k), s) for k in (1, 2, 3)]
        + [(fp, s)]
    )
    sends = []

    def go(copy):
        copy.start()
        sends.append(copy)

    for i, k in enumerate(NEAR_FIRST):
        go(remote(w.at[0], wg.at[0, s], wss.at[0, 0, i], wrs.at[0, k, 0], f, ys(k)))
        go(remote(w.at[1], wg.at[1, s], wss.at[1, 0, i], wrs.at[1, k, 0], f, zs(k)))
    go(remote(v, vg.at[f % 2], vss, vrs, fp, s))
    for i, k in enumerate(NEAR_FIRST):
        go(remote(t, tg.at[f], tss.at[0, i], trs.at[0, k], xs(k), s))
    go(remote(t, tg.at[f], tss.at[1, 0], trs.at[1, 0], fp, s))
    for i, k in enumerate(NEAR_FIRST):
        go(remote(w.at[0], wg.at[0, s], wss.at[0, 1, i], wrs.at[0, 0, k], f, zs(k)))
        go(remote(w.at[1], wg.at[1, s], wss.at[1, 1, i], wrs.at[1, 0, k], f, ys(k)))
    own = [
        pltpu.make_async_copy(w.at[0], wg.at[0, s], local.at[0]),
        pltpu.make_async_copy(w.at[1], wg.at[1, s], local.at[1]),
        pltpu.make_async_copy(t, tg.at[f], local.at[2]),
        pltpu.make_async_copy(v, vg.at[f % 2], local.at[3]),
    ]
    for copy in own:
        copy.start()

    def landed(dst, recv):
        remote(dst, dst, vss, recv, fp, s).wait_recv()

    for j in NEAR_FIRST:
        a, b = ys(4 - j), zs(4 - j)
        landed(wg.at[0, a], wrs.at[0, j, 0])
        for i, k in enumerate(NEAR_FIRST):
            go(remote(wg.at[0, a], wg.at[0, a], wss.at[0, 1 + j, i], wrs.at[0, j, k], f, zs(k)))
        landed(wg.at[1, b], wrs.at[1, j, 0])
        for i, k in enumerate(NEAR_FIRST):
            go(remote(wg.at[1, b], wg.at[1, b], wss.at[1, 1 + j, i], wrs.at[1, j, k], f, ys(k)))
    for j in NEAR_FIRST:
        fs = xs(4 - j)
        landed(tg.at[fs], trs.at[0, j])
        go(remote(tg.at[fs], tg.at[fs], tss.at[1, j], trs.at[1, j], fp, s))
    for j in range(4):
        landed(tg.at[(f // 2 + 4 - j) % 4 * 2 + 1 - f % 2], trs.at[1, j])
    landed(vg.at[fp % 2], vrs)
    for j in range(4):
        for k in (1, 2, 3):
            a = ys(4 - j) // 4 * 4 + zs(4 - k) % 4
            b = ys(4 - k) // 4 * 4 + zs(4 - j) % 4
            landed(wg.at[0, a], wrs.at[0, j, k])
            landed(wg.at[1, b], wrs.at[1, j, k])
    for copy in sends:
        copy.wait_send()
    for copy in own:
        copy.wait()


def gather_inputs(w, t, v):
    shape = jax.ShapeDtypeStruct
    dma = pltpu.SemaphoreType.DMA
    return pl.pallas_call(
        gather_kernel,
        out_shape=(
            shape((2, 16) + w.shape[1:], BF),
            shape((8,) + t.shape, BF),
            shape((2,) + v.shape, BF),
        ),
        in_specs=[pl.BlockSpec(memory_space=pltpu.VMEM)] * 3,
        out_specs=(pl.BlockSpec(memory_space=pl.ANY),) * 3,
        scratch_shapes=[
            dma((4,)),
            dma((2, 5, 3)),
            dma((2, 4, 4)),
            dma((2, 4)),
            dma((2, 4)),
            dma,
            dma,
        ],
        compiler_params=pltpu.CompilerParams(
            collective_id=1, has_side_effects=True, vmem_limit_bytes=16 << 20
        ),
        cost_estimate=pl.CostEstimate(flops=0, bytes_accessed=150_000_000, transcendentals=0),
        name="gather_inputs",
    )(w, t, v)


def vision_kernel(pick, count, slots, wa, wb, gain, bias, bqk, bv, ctx, half, st, nrm, qk, vv, sem):
    core = lax.axis_index("frame") % 2
    copies = [
        pltpu.make_async_copy(slots.at[pick[a]], st.at[pl.ds(a * 256, 256)], sem.at[a])
        for a in range(2)
    ]
    for copy in copies:
        copy.start()
    for copy in copies:
        copy.wait()
    x = st[...].astype(F32)
    centred = x - jnp.mean(x, axis=1, keepdims=True)
    spread = jnp.mean(centred * centred, axis=1, keepdims=True)
    nrm[...] = (centred * lax.rsqrt(spread + 1e-6) * gain[...] + bias[...]).astype(BF)
    half[...] = st[:, pl.ds(pl.multiple_of(core * 640, 128), 640)]

    def project(i, carry):
        rows = pl.ds(pl.multiple_of(i * 128, 128), 128)
        n = nrm[rows, :]
        qk[rows, :] = (jnp.dot(n, wa[...], preferred_element_type=F32) + bqk[...]).astype(BF)
        vv[rows, :] = (jnp.dot(n, wb[...], preferred_element_type=F32) + bv[...]).astype(BF)
        return carry

    lax.fori_loop(0, 4, project, 0)
    for a in range(2):
        live = lax.broadcasted_iota(jnp.int32, (1, 256), 1) < count[a]
        rows = slice(a * 256, a * 256 + 256)
        for h in range(8):
            q = qk[rows, h * 80 : h * 80 + 80]
            k = qk[rows, 640 + h * 80 : 640 + h * 80 + 80]
            v = vv[rows, h * 80 : h * 80 + 80]
            scores = lax.dot_general(
                q, k, (((1,), (1,)), ((), ())), preferred_element_type=F32
            ) * (1.0 / math.sqrt(80))
            scores = jnp.where(live, scores, NEG)
            weights = jnp.exp(scores - jnp.max(scores, axis=1, keepdims=True))
            prob = (weights / jnp.sum(weights, axis=1, keepdims=True)).astype(BF)
            ctx[rows, h * 80 : h * 80 + 80] = jnp.dot(
                prob, v, preferred_element_type=F32
            ).astype(BF)


def vision(pick, count, slots, wa, wb, gain, bias, bqk, bv):
    shape = jax.ShapeDtypeStruct
    smem = pl.BlockSpec(memory_space=pltpu.SMEM)
    vmem = pl.BlockSpec(memory_space=pltpu.VMEM)
    return pl.pallas_call(
        vision_kernel,
        out_shape=(shape((512, 640), BF), shape((512, 640), BF)),
        in_specs=[smem, smem, pl.BlockSpec(memory_space=pl.ANY)] + [vmem] * 6,
        out_specs=(vmem, vmem),
        scratch_shapes=[
            pltpu.VMEM((512, 1280), BF),
            pltpu.VMEM((512, 1280), BF),
            pltpu.VMEM((512, 1280), BF),
            pltpu.VMEM((512, 640), BF),
            pltpu.SemaphoreType.DMA((2,)),
        ],
        compiler_params=pltpu.CompilerParams(vmem_limit_bytes=32 << 20),
        cost_estimate=pl.CostEstimate(
            flops=2_900_000_000, bytes_accessed=9_000_000, transcendentals=1_100_000
        ),
        name="vision",
    )(pick, count, slots, wa, wb, gain, bias, bqk, bv)


def token_kernel(tok, out, local, sss, srs, xss, xrs, pss, prs, land):
    f, s, xs, ys, zs, fp = places()

    def seq_at(k):
        return (s + k) % 16

    greet(
        [(f, seq_at(k)) for k in range(1, 16)] + [(xs(k), s) for k in (1, 2, 3)] + [(fp, s)]
    )
    sends = []

    def go(copy):
        copy.start()
        sends.append(copy)

    for k in range(1, 16):
        go(remote(tok.at[seq_at(k)], land.at[s], sss.at[k], srs.at[k], f, seq_at(k)))
    own = pltpu.make_async_copy(tok.at[s], land.at[s], local.at[0])
    own.start()
    own.wait()

    def landed(dst, recv):
        remote(dst, dst, sss.at[0], recv, fp, s).wait_recv()

    for k in range(1, 16):
        landed(land.at[seq_at(16 - k)], srs.at[k])
    mine = pltpu.make_async_copy(land, out.at[f], local.at[1])
    mine.start()
    for i, k in enumerate(NEAR_FIRST):
        go(remote(land, out.at[f], xss.at[i], xrs.at[k], xs(k), s))
    go(remote(land, out.at[f], pss.at[0], prs.at[0], fp, s))
    for j in NEAR_FIRST:
        fs = xs(4 - j)
        landed(out.at[fs], xrs.at[j])
        go(remote(out.at[fs], out.at[fs], pss.at[j], prs.at[j], fp, s))
    for j in range(4):
        landed(out.at[(f // 2 + 4 - j) % 4 * 2 + 1 - f % 2], prs.at[j])
    for copy in sends:
        copy.wait_send()
    mine.wait()


def exchange_tokens(tok):
    dma = pltpu.SemaphoreType.DMA
    vmem = pl.BlockSpec(memory_space=pltpu.VMEM)
    return pl.pallas_call(
        token_kernel,
        out_shape=jax.ShapeDtypeStruct((8,) + tok.shape, BF),
        in_specs=[vmem],
        out_specs=vmem,
        scratch_shapes=[
            dma((2,)),
            dma((16,)),
            dma((16,)),
            dma((3,)),
            dma((4,)),
            dma((4,)),
            dma((4,)),
            pltpu.VMEM(tok.shape, BF),
        ],
        compiler_params=pltpu.CompilerParams(
            collective_id=2, has_side_effects=True, vmem_limit_bytes=16 << 20
        ),
        cost_estimate=pl.CostEstimate(flops=0, bytes_accessed=50_000_000, transcendentals=0),
        name="exchange_tokens",
    )(tok)


def attend(q_ref, acc, top, den, kv, tile, keys, base, inc):
    scores = lax.dot_general(
        q_ref[tile], kv[:keys, :128], (((1,), (1,)), ((), ())), preferred_element_type=F32
    )
    if base is not None:
        row = lax.broadcasted_iota(jnp.int32, (512, 1), 0) % 256
        col = lax.broadcasted_iota(jnp.int32, (1, keys), 1)
        row = row % 32 * 8 + row // 32 + base + inc
        col = col // 256 * 256 + col % 32 * 8 + col % 256 // 32
        scores = jnp.where(col < row, scores, NEG)
    old = top[tile]
    new = jnp.maximum(old, jnp.max(scores, axis=1, keepdims=True))
    fade = jnp.exp2(old - new)
    weights = jnp.exp2(scores - new[:, :1]).astype(BF)
    top[tile] = new
    wide = jnp.concatenate([kv[:keys, 128:], jnp.ones((keys, 128), BF)], axis=1)
    added = jnp.dot(weights, wide, preferred_element_type=F32)
    den[tile] = den[tile] * fade + added[:, 128:]
    acc[tile] = acc[tile] * fade + added[:, :128]


def by_distance(i):
    return i + i // 2 - i // 3 * 2


def attention_kernel(q, own, out, kv, acc, top, den, ctx, local, ss, fs, rs, css, crs):
    f, s, xs, ys, zs, fp = places()
    y, z = s // 4, s % 4
    greet(
        [(f, ys(k)) for k in (1, 2, 3)]
        + [(f, zs(k)) for k in (1, 2, 3)]
        + [(xs(k), s) for k in (1, 2, 3)]
    )
    sends = []

    def go(copy):
        copy.start()
        sends.append(copy)

    for i, k in enumerate(NEAR_FIRST):
        go(remote(own.at[0], kv.at[0, s], ss.at[0, 0, i], rs.at[0, k, 0], f, ys(k)))
        go(remote(own.at[1], kv.at[1, s], ss.at[1, 0, i], rs.at[1, k, 0], f, zs(k)))
    for i, k in enumerate(NEAR_FIRST):
        go(remote(own.at[0], kv.at[0, s], ss.at[0, 1, i], rs.at[0, 0, k], f, zs(k)))
        go(remote(own.at[1], kv.at[1, s], ss.at[1, 1, i], rs.at[1, 0, k], f, ys(k)))
    kv[0, s] = own[0]
    kv[1, s] = own[1]
    top[...] = jnp.full_like(top, NEG)
    den[...] = jnp.zeros_like(den)
    acc[...] = jnp.zeros_like(acc)

    def step(i, carry):
        j = by_distance(jnp.where(i < 4, i, (i - 4) // 3))
        k = by_distance(jnp.where(i < 4, 0, (i - 4) % 3 + 1))
        a = (y + 4 - j) % 4 * 4 + (z + 4 - k) % 4
        b = (y + 4 - k) % 4 * 4 + (z + 4 - j) % 4

        @pl.when(i > 0)
        def _():
            remote(kv.at[0, a], kv.at[0, a], ss.at[0, 0, 0], rs.at[0, j, k], f, s).wait_recv()
            remote(kv.at[1, b], kv.at[1, b], ss.at[0, 0, 0], rs.at[1, j, k], f, s).wait_recv()

        @pl.when((i > 0) & (i < 4))
        def _():
            for n, d in enumerate(NEAR_FIRST):
                remote(
                    kv.at[0, a], kv.at[0, a], fs.at[0, j, n], rs.at[0, j, d], f, zs(d)
                ).start()
                remote(
                    kv.at[1, b], kv.at[1, b], fs.at[1, j, n], rs.at[1, j, d], f, ys(d)
                ).start()

        at = functools.partial(attend, q, acc, top, den)
        inc = jnp.where(a <= s, 1, 0)
        at(kv.at[0, a], 0, 256, 0, inc)
        at(kv.at[0, a], 1, 512, 256, inc)
        at(kv.at[0, a], 2, 512, None, inc)
        at(kv.at[0, a], 3, 512, None, inc)
        inc = jnp.where(b <= s, 1, 0)
        at(kv.at[1, b], 2, 256, 0, inc)
        at(kv.at[1, b], 3, 512, 256, inc)
        return carry

    lax.fori_loop(0, 16, step, 0)
    for tile in range(4):
        block = (acc[tile] / den[tile]).astype(BF)
        for head in range(2):
            for owner in range(8):
                start = head * 256 + owner * 32
                ctx[owner // 2, owner % 2, tile, head] = block[start : start + 32]
    for copy in sends:
        copy.wait_send()

    def drain(j, carry):
        for n in range(3):
            for h in range(2):
                remote(own.at[0], kv.at[0, s], fs.at[h, j, n], rs.at[0, 0, 0], f, s).wait_send()
        return carry

    lax.fori_loop(1, 4, drain, 0)
    x = f // 2
    last = []
    for i, k in enumerate(NEAR_FIRST):
        copy = remote(ctx.at[(x + k) % 4], out.at[x], css.at[i], crs.at[k], xs(k), s)
        copy.start()
        last.append(copy)
    keep = pltpu.make_async_copy(ctx.at[x], out.at[x], local)
    keep.start()
    for k in (1, 2, 3):
        here = out.at[(x + 4 - k) % 4]
        remote(here, here, css.at[0], crs.at[k], f, s).wait_recv()
    for copy in last:
        copy.wait_send()
    keep.wait()


def attention(q, own):
    dma = pltpu.SemaphoreType.DMA
    vmem = pl.BlockSpec(memory_space=pltpu.VMEM)
    state = pltpu.VMEM((4, 512, 128), F32)
    return pl.pallas_call(
        attention_kernel,
        out_shape=jax.ShapeDtypeStruct((4, 2, 4, 2, 32, 128), BF),
        in_specs=[vmem, vmem],
        out_specs=vmem,
        scratch_shapes=[
            pltpu.VMEM((2, 16, 512, 256), BF),
            state,
            state,
            state,
            pltpu.VMEM((4, 2, 4, 2, 32, 128), BF),
            dma,
            dma((2, 2, 3)),
            dma((2, 4, 3)),
            dma((2, 4, 4)),
            dma((3,)),
            dma((4,)),
        ],
        compiler_params=pltpu.CompilerParams(
            collective_id=3, has_side_effects=True, vmem_limit_bytes=40 << 20
        ),
        cost_estimate=pl.CostEstimate(
            flops=24_000_000_000, bytes_accessed=9_000_000, transcendentals=20_000_000
        ),
        name="attention",
    )(q, own)


def swap_cores(value):
    return lax.ppermute(value, "frame", [(i, i ^ 1) for i in range(8)])


def per_device(
    vit_states,
    frame_slot,
    patch_count,
    vis_start,
    text_embed,
    vit_ln_gain,
    vit_ln_bias,
    vit_qkv_w,
    vit_qkv_b,
    vit_out_w,
    vit_out_b,
    proj_w,
    proj_b,
    attn_gain,
    wq,
    wk,
    wv,
    wo,
):
    f = lax.axis_index("frame")
    s = lax.axis_index("seq")
    core = f % 2
    holder = frame_slot // 2
    pair = holder // 32 * 16 + holder % 16
    order = holder // 16 % 2 * 2 + frame_slot % 2
    before = (pair[:, None] == pair[None, :]) & (order[None, :] < order[:, None])
    rank = jnp.sum(before.astype(jnp.int32), axis=1)
    here = (pair == f // 2 * 16 + s)[None, :] & (rank[None, :] == jnp.arange(2)[:, None])
    facts = jnp.stack([order, patch_count, vis_start])
    facts = jnp.sum(jnp.where(here[None], facts[:, None, :], 0), axis=2)
    pick, count, start = facts[0], facts[1], facts[2]

    def half_of(a):
        return jnp.where(core == 0, a[..., :640], a[..., 640:])

    qw, kw, vw = jnp.split(vit_qkv_w, 3, axis=1)
    qb, kb, vb = jnp.split(vit_qkv_b, 3)
    shard = jnp.stack(
        [
            jnp.concatenate([half_of(qw), half_of(kw)], axis=1),
            jnp.concatenate([half_of(vw), half_of(vit_out_w)], axis=1),
        ]
    )
    text = text_embed.reshape(128, 4096).astype(F32)
    text = (
        text * lax.rsqrt(jnp.mean(text * text, axis=1, keepdims=True) + 1e-5) * attn_gain
    ).astype(BF)
    weights, texts, slots = gather_inputs(shard, text, vit_states)
    wo_late = lax.optimization_barrier((wo, weights))[0]
    wo_parts = [wo] + [
        lax.ppermute(wo_late, "frame", [(i, i ^ k) for i in range(8)]) for k in (2, 6, 4)
    ]
    weights = weights.reshape(2, 1280, 1280)
    ctx, states_half = vision(
        pick,
        count,
        slots.reshape(4, 256, 1280),
        weights[0],
        weights[1, :, :640],
        vit_ln_gain[None],
        vit_ln_bias[None],
        jnp.concatenate([half_of(qb), half_of(kb)])[None],
        half_of(vb)[None],
    )
    other = swap_cores(ctx)
    ctx = jnp.where(
        core == 0, jnp.concatenate([ctx, other], axis=1), jnp.concatenate([other, ctx], axis=1)
    )
    attended = jnp.dot(ctx, weights[1, :, 640:], preferred_element_type=F32)
    hidden = (states_half.astype(F32) + attended + half_of(vit_out_b)).astype(BF)
    pooled = jnp.mean(hidden.astype(F32).reshape(128, 4, 640), axis=1).astype(BF)
    other = swap_cores(pooled)
    whole = jnp.where(
        core == 0,
        jnp.concatenate([pooled, other], axis=1),
        jnp.concatenate([other, pooled], axis=1),
    )
    seen = jnp.dot(whole, proj_w, preferred_element_type=F32) + proj_b
    scale = lax.rsqrt(jnp.mean(seen * seen, axis=1, keepdims=True) + 1e-5)
    lane = jnp.arange(128)[None, :]
    tokens = jnp.concatenate(
        [(pooled.astype(F32) * scale).astype(BF), jnp.where(lane == 0, scale, 0.0).astype(BF)],
        axis=1,
    )
    want = jnp.arange(128)
    frame_of = want // 4 % 2
    token = (want // 8 - jnp.where(frame_of == 0, start[0], start[1])) % 16 + want % 4 * 16
    taken = (frame_of * 64 + token)[:, None] == jnp.arange(128)[None, :]
    tokens = jnp.dot(taken.astype(BF), tokens, preferred_element_type=F32).astype(BF)
    table = exchange_tokens(tokens.reshape(16, 8, 768)).reshape(4, 2, 128, 768)
    wide = jnp.concatenate([wq, wk, wv], axis=1)
    gained = (attn_gain[:, None] * wide.astype(F32)).astype(BF)
    folded = jnp.dot(proj_w, gained, preferred_element_type=F32).astype(BF)
    bias_high = proj_b.astype(BF)
    bias_low = (proj_b - bias_high.astype(F32)).astype(BF)
    bias = jnp.sum(
        jnp.dot(jnp.stack([bias_high, bias_low]), gained, preferred_element_type=F32),
        axis=0,
        keepdims=True,
    )
    bias = jnp.where(lane.T == 0, bias, 0.0).astype(BF)
    low = jnp.concatenate([folded[:640], bias], axis=0)
    high = jnp.concatenate([folded[640:], jnp.zeros_like(bias)], axis=0)
    visual = (
        jnp.dot(table[:, 0].reshape(512, 768), low, preferred_element_type=F32)
        + jnp.dot(table[:, 1].reshape(512, 768), high, preferred_element_type=F32)
    ).astype(BF)
    owner = jnp.arange(8)[None, :, None]
    frame = jnp.arange(128).reshape(4, 1, 32)
    within = frame * 128 + owner * 16 + s - vis_start.reshape(4, 1, 32)
    live = (within >= 0) & (within < patch_count.reshape(4, 1, 32) // 4)
    source = (pair * 8 + rank * 4).reshape(4, 1, 32) + within // 16
    source = jnp.where(live, source, -1).reshape(1024, 1)
    chosen = (source == jnp.arange(512)[None, :]).astype(BF)
    visual = jnp.dot(chosen, visual, preferred_element_type=F32)
    texts = texts.reshape(8, 4, 32, 4096).transpose(1, 0, 2, 3).reshape(1024, 4096)
    plain = jnp.dot(texts, wide, preferred_element_type=F32)
    projected = jnp.where(source >= 0, visual, plain)
    position = (frame * 128 + owner * 16 + s).reshape(1024, 1).astype(F32)
    exponents = jnp.arange(0, 128, 2).astype(F32) / 128
    angles = position * jnp.power(F32(ROPE_THETA), -exponents)[None, :]
    cosine, sine = jnp.cos(angles), jnp.sin(angles)

    def rotate(v):
        a, b = v[:, :64], v[:, 64:]
        return jnp.concatenate([a * cosine - b * sine, b * cosine + a * sine], axis=1)

    factor = math.log2(math.e) / math.sqrt(128)
    queries = jnp.stack(
        [(rotate(projected[:, h * 128 : h * 128 + 128]) * factor).astype(BF) for h in range(2)]
    )
    queries = queries.reshape(2, 4, 256, 128).transpose(1, 0, 2, 3).reshape(4, 512, 128)
    own = jnp.concatenate(
        [rotate(projected[:, 256:384]).astype(BF), projected[:, 384:].astype(BF)], axis=1
    )
    ctx = attention(queries, own.reshape(2, 512, 256))
    ctx = ctx.transpose(1, 2, 4, 0, 3, 5).reshape(256, 4, 256)
    x = f // 2
    partial = jnp.zeros((256, 4096), F32)
    for k, part in zip((0, 1, 3, 2), wo_parts):
        columns = lax.dynamic_index_in_dim(ctx, x ^ k, axis=1, keepdims=False)
        partial = partial + jnp.dot(columns, part, preferred_element_type=F32)
    keep = jnp.where(core == 0, partial[:128], partial[128:])
    give = jnp.where(core == 0, partial[128:], partial[:128]).astype(BF)
    mixed = (keep + swap_cores(give).astype(F32)).astype(BF)
    return mixed.reshape(128, 1, 4096)


def solution(mesh):
    return jax.shard_map(
        per_device,
        mesh=mesh,
        in_specs=(
            P(("frame", "seq"), None, None),
            P(),
            P(),
            P(),
            P(None, ("frame", "seq"), None),
            P(),
            P(),
            P("seq", None),
            P(),
            P("seq", None),
            P(),
            P(),
            P(),
            P(),
            P(None, "frame"),
            P(None, "frame"),
            P(None, "frame"),
            P("frame", None),
        ),
        out_specs=P(None, ("frame", "seq"), None),
        check_vma=False,
    )
```

time: 681 us -> 286 us (0.42)
  waiting for transfers between devices: 256 us -> 2.37 us
  matrix products: 263 us -> 57.5 us
  Pallas kernels: 0 us -> 164 us
  other arithmetic: 76.8 us -> 10.1 us
  between operations: 20.1 us -> 0.89 us
  local copies, waits for them, and re-layouts: 52.4 us -> 33.6 us
    dot_general x41 -> x12, matrix products: 263 us -> 57.5 us  [the longest x1 23.9 us: per_device(): folded = jnp.dot(proj_w, gained, preferred_element_type=F32).astype(BF)]
    all_gather x4 -> x0, waiting for transfers between devices: 191 us -> none  [the longest x1 60.5 us: per_device(): lax.all_gather(vit_qkv_w, 'seq', axis=0, tiled=True)]
    pallas_call x0 -> x4, Pallas kernels: none -> 164 us  [the longest x1 70.8 us: attention(): pl.pallas_call(attention_kernel, out_shape=jax.ShapeDtypeStruct((4, 2, 4,...]
    reduce_scatter x1 -> x0, waiting for transfers between devices: 51.8 us -> none  [per_device(): lax.psum_scatter(jnp.dot(context_tok, wo, preferred_element_type=jnp.floa...]
    reduce_sum x21 -> x4, other arithmetic: 41 us -> 2.7 us  [the longest x1 1.61 us: per_device(): jnp.mean(text * text, axis=1, keepdims=True) + 1e-05]
    all_to_all x1 -> x0, waiting for transfers between devices: 11.6 us -> none  [per_device(): lax.all_to_all(outgoing, ('frame', 'seq'), split_axis=0, concat_axis=0, t...]
    le x16 -> x0, other arithmetic: 10.4 us -> none  [visit(): allowed = key_positions[None, :] <= group_positions[:, None]]
    ppermute x1 -> x6, starting transfers between devices: 1.46 us -> 11.8 us  [the longest x3 8.52 us: swap_cores(): return lax.ppermute(value, 'frame', [(i, i ^ 1) for i in range(8)])]
  transfers between devices with their start and end apart: 7 -> 6, of which waited for: 6 -> 2; matrix products, arithmetic and copies ran while one was open for 7% -> 29% of each run, Pallas kernels for 0% -> 38%
where the time goes in v1:
time: 286 us; the launch traced here: 280 us
  Pallas kernels  164 us (57%)
  matrix products  57.5 us (20%)
  local copies, waits for them, and re-layouts  33.6 us (12%)
  starting transfers between devices  11.8 us (4%)
  other arithmetic  10.1 us (4%)
    pallas_call x1, Pallas kernels, attention(): pl.pallas_call(attention_kernel, out_shape=jax.ShapeDtypeStruct((4, 2, 4,...  70.8 us
    pallas_call x1, Pallas kernels, gather_inputs(): pl.pallas_call(gather_kernel, out_shape=(shape((2, 16) + w.shape[1:], BF)...  56.9 us
    dot_general x1, matrix products, per_device(): folded = jnp.dot(proj_w, gained, preferred_element_type=F32).astype(BF)  23.9 us
    pallas_call x1, Pallas kernels, exchange_tokens(): pl.pallas_call(token_kernel, out_shape=jax.ShapeDtypeStruct((8,) + tok.sh...  21.1 us
    pallas_call x1, Pallas kernels, vision(): pl.pallas_call(vision_kernel, out_shape=(shape((512, 640), BF), shape((51...  15.2 us
    unnamed x50, local copies, waits for them, and re-layouts  13.2 us
    dot_general x4, matrix products, per_device(): partial = partial + jnp.dot(columns, part, preferred_element_type=F32)  9.59 us
    ppermute x3, starting transfers between devices, swap_cores(): return lax.ppermute(value, 'frame', [(i, i ^ 1) for i in range(8)])  8.52 us
  transfers between devices with their start and end apart: 6, of which 2 were waited for; matrix products, arithmetic and copies ran while one was open for 29% of the time, Pallas kernels for 38%

profile of v1, /device:TPU:1, one launch (start us, length us, event | category | flops | bytes accessed | tf_op | source)
XLA Modules:
  0.0 280.3 jit_solution(9378085674232481112)
XLA Ops:
  0.0 1.6 fusion.3
  1.6 1.3 slice_select_fusion.3
  3.0 0.3 fusion.5.t
  3.4 0.9 copy-done.2
  4.2 56.9 %gather_inputs.1 = (bf16[2,16,80,1280]{3,2,1,0:T(8,128)(2,1)S(1)}, bf16[8,128,4096]{2,1,0:T(8,128)(2,1)S(1)}, bf16[2,2,256,1280]{3,2,1,0:T(8,128)(2,1)S(1)}) custom-call(bf16[2,80,1280]{2,1,0:T(8,128)(2,1)S(1)} %pad_maximum_fusion.2.w, bf16[128,4096]{1,0:T(8,128)(2,1)S(1)} %fusion.5.t, bf16[2,256,1280]{2,1,0:T(8,128)(2,1)S(1)} %copy-done.2), custom_call_target="tpu_custom_call" | custom-call | bytes 150000000 | tf_op jit(solution)/shard_map/gather_inputs/pallas_call | solution.py:123
  61.2 3.3 %copy-done = bf16[8,128,4096]{2,1,0:T(8,128)(2,1)} copy-done((bf16[8,128,4096]{2,1,0:T(8,128)(2,1)}, bf16[8,128,4096]{2,1,0:T(8,128)(2,1)S(1)}, u32[]{:S(2)}) %copy-start) | copy-done | bytes 8388632
  64.4 2.7 copy-done.1
  67.2 1.6 copy-done.3
  68.7 0.3 collective-permute-start.4
  69.0 1.2 collective-permute-start.2
  70.2 1.8 collective-permute-start.3
  72.0 2.2 slice.150
  74.3 0.2 convert_reduce_fusion
  74.5 0.1 select_reduce_fusion
  74.7 1.8 slice_bitcast_fusion.2.wb
  76.6 15.2 %vision.1 = (bf16[512,640]{1,0:T(8,128)(2,1)}, bf16[512,640]{1,0:T(8,128)(2,1)S(1)}) custom-call(s32[2]{0:T(128)S(1)} %get-tuple-element.46.pick, s32[2]{0:T(128)S(1)} %get-tuple-element.45.count, bf16[4,256,1280]{2,1,0:T(8,128)(2,1)S(1)} %bitcast.87, bf16[1280,1280]{1,0:T(8,128)(2,1)S(1)} %bitcast.83, bf16[1280,640]{1,0:T(8,128)(2,1)S(1)} %slice_bitcast_fusion.2.wb, ...), custom_call_target="tpu_custom_call" | custom-call | flops 2900000000 | bytes 9000000 | tf_op jit(solution)/shard_map/vision/pallas_call | solution.py:195
  91.8 0.8 copy-done.5
  92.7 1.1 collective-permute-start
  94.0 7.9 %copy.31 = bf16[8,4,32,4096]{3,2,0,1:T(8,128)(2,1)} copy(bf16[8,4,32,4096]{3,2,1,0:T(8,128)(2,1)} %bitcast.79) | data formatting | bytes 16777216 | tf_op jit(solution)/shard_map/reshape | solution.py:551
  101.8 0.2 constant_dynamic-update-slice_fusion.2
  102.1 1.6 constant_dynamic-update-slice_fusion.1
  103.7 1.9 constant_dynamic-update-slice_fusion
  105.6 1.9 copy-done.11
  107.6 6.0 %fusion.111 = f32[1024,512]{0,1:T(8,128)} fusion(bf16[1024,4096]{1,0:T(8,128)(2,1)S(1)} %bitcast.88, bf16[4096,512]{1,0:T(8,128)(2,1)S(1)} %constant_dynamic-update-slice_fusion), kind=kOutput, calls=%fused_computation.208 | convolution fusion | flops 4294967296 | bytes 14680064 | tf_op jit(solution)/shard_map/dot_general | solution.py:552
  113.6 23.9 %fusion.2 = bf16[1280,512]{0,1:T(8,128)(2,1)S(1)} fusion(bf16[1280,4096]{1,0:T(8,128)(2,1)} %param.29, bf16[4096,512]{1,0:T(8,128)(2,1)} %copy-done.11, f32[4096]{0:T(1024)S(1)} %copy-done.16), kind=kOutput, calls=%fused_computation.7 | convolution fusion | flops 5375655936 | bytes 16007168 | tf_op jit(solution)/shard_map/dot_general | solution.py:528
  137.4 0.1 add.268
  137.9 2.8 fusion.23
  140.7 0.6 fusion.110
  141.3 0.1 select_convert_fusion.1
  141.4 0.1 fusion.109
  141.6 0.2 copy-done.6
  141.7 4.6 %fusion.14 = f32[512,640]{1,0:T(8,128)} fusion(bf16[2,1280,1280]{2,1,0:T(8,128)(2,1)} %bitcast.82, bf16[512,640]{1,0:T(8,128)(2,1)} %collective-permute-done, bf16[512,640]{1,0:T(8,128)(2,1)} %get-tuple-element.14, bf16[512,640]{1,0:T(8,128)(2,1)S(1)} %copy-done.6, pred[]{:T(512)S(6)} %eq.111, f32[640]{0:T(1024)S(1)} %slice_select_fusion.4), kind=kOutput, calls=%fused_computation.27 | convolution fusion | flops 846397440 | bytes 4917761 | tf_op jit(solution)/shard_map/dot_general | solution.py:504
  146.3 1.7 reshape.463
  148.0 0.8 reduce_sum.57
  148.8 0.1 collective-permute-start.1
  149.0 1.2 fusion.93
  150.3 5.6 %fusion.11 = f32[128]{0:T(128)S(1)} fusion(bf16[1280,4096]{1,0:T(8,128)(2,1)} %param.29, f32[4096]{0:T(1024)S(1)} %copy-done.17, bf16[128,640]{1,0:T(8,128)(2,1)S(1)} %collective-permute-done.1, bf16[128,640]{1,0:T(8,128)(2,1)S(1)} %multiply_convert_fusion.6, pred[]{:T(512)S(6)} %eq.111), kind=kOutput, calls=%fused_computation.23 | convolution fusion | flops 1345224576 | bytes 10830337 | tf_op jit(solution)/shard_map/dot_general | solution.py:513
  155.9 0.1 select_convert_fusion.2
  156.0 0.1 multiply_convert_fusion.5
  156.1 0.2 fusion.22.tok
  156.4 21.1 %exchange_tokens.1 = bf16[8,16,8,768]{3,2,1,0:T(8,128)(2,1)S(1)} custom-call(bf16[16,8,768]{2,1,0:T(8,128)(2,1)S(1)} %fusion.22.tok), custom_call_target="tpu_custom_call" | custom-call | bytes 50000000 | tf_op jit(solution)/shard_map/exchange_tokens/pallas_call | solution.py:260
  177.5 0.1 fusion.108
  177.6 1.6 fusion.26
  179.2 3.2 %fusion.9 = f32[1024,512]{0,1:T(8,128)S(1)} fusion(f32[1024,512]{0,1:T(8,128)} %fusion.111, f32[512,512]{1,0:T(8,128)} %fusion.26, bf16[512,768]{1,0:T(8,128)(2,1)S(1)} %bitcast.89, s32[1024]{0:T(1024)S(1)} %get-tuple-element.18, pred[1024]{0:T(1024)(128)(4,1)S(1)} %get-tuple-element.17, bf16[640,512]{0,1:T(8,128)(2,1)S(1)} %get-tuple-element.33), kind=kOutput, calls=%fused_computation.21 | convolution fusion | flops 941096960 | bytes 6689792 | tf_op jit(solution)/shard_map/dot_general | solution.py:550
  182.4 0.7 slice.239
  183.2 2.0 fusion.57
  185.2 0.2 copy.41
  185.4 0.2 copy.40
  185.6 1.1 copy.39
  186.7 0.2 copy.38
  187.0 0.2 copy.36
  187.2 0.2 fusion.33
  187.4 0.2 fusion.32
  187.7 70.8 %attention.1 = bf16[4,2,4,2,32,128]{5,4,3,2,1,0:T(8,128)(2,1)S(1)} custom-call(bf16[4,512,128]{2,1,0:T(8,128)(2,1)S(1)} %bitcast.85, bf16[2,512,256]{2,1,0:T(8,128)(2,1)S(1)} %bitcast.84), custom_call_target="tpu_custom_call" | custom-call | flops 24000000000 | bytes 9000000 | tf_op jit(solution)/shard_map/attention/pallas_call | solution.py:403
  258.5 0.5 copy.37
  259.1 0.3 reshape.459
  259.4 2.3 fusion.67
  261.7 2.3 fusion.63
  264.0 2.4 convolution_add_fusion.1
  266.5 2.5 fusion
  269.0 0.2 select_convert_fusion
  269.2 7.3 %collective-permute-start.5 = (bf16[128,4096]{1,0:T(8,128)(2,1)S(1)}, bf16[128,4096]{1,0:T(8,128)(2,1)S(1)}, u32[]{:S(2)}, u32[]{:S(2)}) collective-permute-start(bf16[128,4096]{1,0:T(8,128)(2,1)S(1)} %select_convert_fusion), channel_id=1, source_target_pairs={{0,16},{16,0},{32,48},{48,32},{64,80},{80,64},{96,112},{112,96},{1... | collective-permute-start | bytes 3145736 | tf_op jit(solution)/shard_map/ppermute | solution.py:432
  276.5 2.3 collective-permute-done.5
  278.8 1.3 fusion.24
  (85 shorter events, 1.1 us)
Async XLA Ops:
  0.0 3.0 %copy-start.8 = (bf16[128,1,4096]{2,0,1:T(8,128)(2,1)S(1)}, bf16[128,1,4096]{2,0,1:T(8,128)(2,1)}, u32[]{:S(2)}) copy-start(bf16[128,1,4096]{2,0,1:T(8,128)(2,1)} %param.22) | copy-start | bytes 3145732
  0.0 3.0 %copy-start.16 = (f32[4096]{0:T(1024)S(1)}, f32[4096]{0:T(1024)}, u32[]{:S(2)}) copy-start(f32[4096]{0:T(1024)} %param.31) | copy-start | bytes 49156
  2.9 1.3 copy-start.2
  61.1 3.3 %copy-start = (bf16[8,128,4096]{2,1,0:T(8,128)(2,1)}, bf16[8,128,4096]{2,1,0:T(8,128)(2,1)S(1)}, u32[]{:S(2)}) copy-start(bf16[8,128,4096]{2,1,0:T(8,128)(2,1)S(1)} %get-tuple-element.15) | copy-start | bytes 25165828
  64.4 2.7 copy-start.1
  67.2 1.6 copy-start.3
  68.7 193.0 %collective-permute-start.4 = (bf16[256,4096]{1,0:T(8,128)(2,1)}, bf16[256,4096]{1,0:T(8,128)(2,1)}, u32[]{:S(2)}, u32[]{:S(2)}) collective-permute-start(bf16[256,4096]{1,0:T(8,128)(2,1)} %param.35), channel_id=1, source_target_pairs={{0,64},{16,80},{32,96},{48,112},{64,0},{80,16},{96,32},{112,48},{1... | collective-permute-start | bytes 6291464 | tf_op jit(solution)/shard_map/ppermute | solution.py:486
  69.0 195.0 %collective-permute-start.2 = (bf16[256,4096]{1,0:T(8,128)(2,1)}, bf16[256,4096]{1,0:T(8,128)(2,1)}, u32[]{:S(2)}, u32[]{:S(2)}) collective-permute-start(bf16[256,4096]{1,0:T(8,128)(2,1)} %param.35), channel_id=1, source_target_pairs={{0,32},{16,48},{32,0},{48,16},{64,96},{80,112},{96,64},{112,80},{1... | collective-permute-start | bytes 6291464 | tf_op jit(solution)/shard_map/ppermute | solution.py:486
  70.2 196.3 %collective-permute-start.3 = (bf16[256,4096]{1,0:T(8,128)(2,1)}, bf16[256,4096]{1,0:T(8,128)(2,1)}, u32[]{:S(2)}, u32[]{:S(2)}) collective-permute-start(bf16[256,4096]{1,0:T(8,128)(2,1)} %param.35), channel_id=1, source_target_pairs={{0,96},{16,112},{32,64},{48,80},{64,32},{80,48},{96,0},{112,16},{1... | collective-permute-start | bytes 6291464 | tf_op jit(solution)/shard_map/ppermute | solution.py:486
  72.0 2.2 copy-start.23
  72.0 2.5 copy-start.21
  72.0 2.5 copy-start.22
  74.2 2.3 copy-start.19
  74.2 2.3 copy-start.20
  74.2 2.3 copy-start.15
  74.3 2.3 copy-start.4
  91.8 0.8 copy-start.5
  92.7 48.9 %collective-permute-start = (bf16[512,640]{1,0:T(8,128)(2,1)}, bf16[512,640]{1,0:T(8,128)(2,1)}, u32[]{:S(2)}, u32[]{:S(2)}) collective-permute-start(bf16[512,640]{1,0:T(8,128)(2,1)} %get-tuple-element.14), channel_id=1, source_target_pairs={{0,16},{16,0},{32,48},{48,32},{64,80},{80,64},{96,112},{112,96},{1... | collective-permute-start | bytes 1966088 | tf_op jit(solution)/shard_map/ppermute | solution.py:432
  94.0 7.9 %copy-start.9 = (bf16[4096,256]{1,0:T(8,128)(2,1)S(1)}, bf16[4096,256]{1,0:T(8,128)(2,1)}, u32[]{:S(2)}) copy-start(bf16[4096,256]{1,0:T(8,128)(2,1)} %param.32) | copy-start | bytes 6291460
  94.0 8.0 %copy-start.18 = (f32[1280]{0:T(1024)S(1)}, f32[1280]{0:T(1024)}, u32[]{:S(2)}) copy-start(f32[1280]{0:T(1024)} %param.28) | copy-start | bytes 15364
  94.0 8.1 %copy-start.17 = (f32[4096]{0:T(1024)S(1)}, f32[4096]{0:T(1024)}, u32[]{:S(2)}) copy-start(f32[4096]{0:T(1024)} %param.30) | copy-start | bytes 49156
  101.8 5.7 %copy-start.7 = (bf16[8,4,32,4096]{3,2,0,1:T(8,128)(2,1)S(1)}, bf16[8,4,32,4096]{3,2,0,1:T(8,128)(2,1)}, u32[]{:S(2)}) copy-start(bf16[8,4,32,4096]{3,2,0,1:T(8,128)(2,1)} %copy.31) | copy-start | bytes 25165828
  105.6 1.9 copy-start.11
  140.6 1.1 copy-start.6
  148.8 1.5 collective-permute-start.1
  185.2 1.6 copy-start.10
  185.2 1.8 copy-start.12
  185.2 1.8 copy-start.13
  185.2 1.8 copy-start.14
  269.2 9.6 %collective-permute-start.5 = (bf16[128,4096]{1,0:T(8,128)(2,1)S(1)}, bf16[128,4096]{1,0:T(8,128)(2,1)S(1)}, u32[]{:S(2)}, u32[]{:S(2)}) collective-permute-start(bf16[128,4096]{1,0:T(8,128)(2,1)S(1)} %select_convert_fusion), channel_id=1, source_target_pairs={{0,16},{16,0},{32,48},{48,32},{64,80},{80,64},{96,112},{112,96},{1... | collective-permute-start | bytes 3145736 | tf_op jit(solution)/shard_map/ppermute | solution.py:432

commit v2 on v1

v2 whole, which is shorter than its diff:
```python
import functools
import math

import jax
import jax.numpy as jnp
from jax import lax
from jax.experimental import pallas as pl
from jax.experimental.pallas import tpu as pltpu
from jax.sharding import PartitionSpec as P

MESH = pl.DeviceIdType.MESH
BF = jnp.bfloat16
F32 = jnp.float32
NEG = -1e30
ROPE_THETA = 500000.0
NEAR_FIRST = (1, 3, 2)


def remote(src, dst, send, recv, f, s):
    return pltpu.make_async_remote_copy(
        src_ref=src,
        dst_ref=dst,
        send_sem=send,
        recv_sem=recv,
        device_id={"frame": f, "seq": s},
        device_id_type=MESH,
    )


def places():
    f = lax.axis_index("frame")
    s = lax.axis_index("seq")
    y, z = s // 4, s % 4

    def along_y(k):
        return (y + k) % 4 * 4 + z

    def along_z(k):
        return y * 4 + (z + k) % 4

    def along_x(k):
        return (f // 2 + k) % 4 * 2 + f % 2

    partner = f + 1 - 2 * (f % 2)
    return f, s, along_x, along_y, along_z, partner


def greet(peers):
    barrier = pltpu.get_barrier_semaphore()
    for f, s in peers:
        pl.semaphore_signal(
            barrier, inc=1, device_id={"frame": f, "seq": s}, device_id_type=MESH
        )
    pl.semaphore_wait(barrier, len(peers))


def turned(row, eye):
    return jnp.sum(jnp.where(eye, row.astype(F32), 0.0), axis=1, keepdims=True).astype(jnp.int32)


def front_kernel(
    slot_r, count_r, start_r, v, qkvw, outw, t, ln_g, ln_b, qkvb, outb, pbias, again, ca, sa, cb, sb, pb,
    proj, wq, wk, wv,
    q_out, kv_out,
    ws, wg, vp, tg, pw, wc, fold, plain, st, nrm, qk, vv, ctx, ctxo, pool, poolo, tok, land, table, col,
    local, wss, wrs, tss, trs, vss, vrs, ess, ers, sss, srs, xss, xrs, pss, prs,
):
    f, s, xs, ys, zs, fp = places()
    core = f % 2

    def seq_at(k):
        return (s + k) % 16

    def lanes(first):
        return pl.ds(pl.multiple_of(first + core * 640, 128), 640)

    def landed(dst, recv):
        remote(dst, dst, vss, recv, fp, s).wait_recv()

    packs = [
        pltpu.make_async_copy(qkvw.at[:, lanes(0)], ws.at[0, :, pl.ds(0, 640)], local.at[0]),
        pltpu.make_async_copy(qkvw.at[:, lanes(1280)], ws.at[0, :, pl.ds(640, 640)], local.at[1]),
        pltpu.make_async_copy(qkvw.at[:, lanes(2560)], ws.at[1, :, pl.ds(0, 640)], local.at[2]),
        pltpu.make_async_copy(outw.at[:, lanes(0)], ws.at[1, :, pl.ds(640, 640)], local.at[3]),
    ]
    loads = [
        pltpu.make_async_copy(wq, wc.at[:, pl.ds(0, 256)], local.at[4]),
        pltpu.make_async_copy(wk, wc.at[:, pl.ds(256, 128)], local.at[5]),
        pltpu.make_async_copy(wv, wc.at[:, pl.ds(384, 128)], local.at[6]),
        pltpu.make_async_copy(proj, pw, local.at[7]),
    ]
    for copy in packs:
        copy.start()
    greet(
        [(f, seq_at(k)) for k in range(1, 16)]
        + [(xs(k), s) for k in (1, 2, 3)]
        + [(fp, s)]
    )
    for copy in packs:
        copy.wait()
    sends = []

    def go(copy):
        copy.start()
        sends.append(copy)

    for i, k in enumerate(NEAR_FIRST):
        go(remote(ws.at[0], wg.at[0, s], wss.at[0, 0, i], wrs.at[0, k, 0], f, ys(k)))
        go(remote(ws.at[1], wg.at[1, s], wss.at[1, 0, i], wrs.at[1, k, 0], f, zs(k)))
    go(remote(v, vp, vss, vrs, fp, s))
    for i, k in enumerate(NEAR_FIRST):
        go(remote(t, tg.at[f], tss.at[0, i], trs.at[0, k], xs(k), s))
    go(remote(t, tg.at[f], tss.at[1, 0], trs.at[1, 0], fp, s))
    for i, k in enumerate(NEAR_FIRST):
        go(remote(ws.at[0], wg.at[0, s], wss.at[0, 1, i], wrs.at[0, 0, k], f, zs(k)))
        go(remote(ws.at[1], wg.at[1, s], wss.at[1, 1, i], wrs.at[1, 0, k], f, ys(k)))
    for copy in loads:
        copy.start()
    wg[0, s] = ws[0]
    wg[1, s] = ws[1]
    slot = slot_r[...]
    holder = slot // 2
    pair = holder // 32 * 16 + holder % 16
    order = holder // 16 % 2 * 2 + slot % 2
    eye = lax.broadcasted_iota(jnp.int32, (128, 128), 0) == lax.broadcasted_iota(
        jnp.int32, (128, 128), 1
    )
    pair_c, order_c = turned(pair, eye), turned(order, eye)
    same = pair_c == pair
    rank = jnp.sum(jnp.where(same & (order_c < order), 1.0, 0.0), axis=0, keepdims=True).astype(
        jnp.int32
    )
    col[:, 0:1] = pair_c * 8 + turned(rank, eye) * 4
    col[:, 1:2] = turned(start_r[...], eye)
    col[:, 2:3] = turned(count_r[...], eye)
    facts = []
    for a in range(2):
        mine = (pair == f // 2 * 16 + s) & (rank == a)
        facts.append(
            [
                jnp.sum(
                    jnp.where(mine, row.astype(F32), 0.0), axis=1, keepdims=True
                ).astype(jnp.int32)
                for row in (order, count_r[...], start_r[...])
            ]
        )
    for copy in loads:
        copy.wait()

    def fold_rows(i, carry):
        rows = pl.ds(pl.multiple_of(i * 128, 128), 128)
        to = pl.ds(pl.multiple_of(i * 128 + i // 5 * 128, 128), 128)
        gained = (pw[rows, :].astype(F32) * again[...]).astype(BF)
        fold[to, :] = jnp.dot(gained, wc[...], preferred_element_type=F32).astype(BF)
        return carry

    def text_rows(source, at):
        plain[:, at] = jnp.dot(source[...], wc[...], preferred_element_type=F32).reshape(4, 32, 512)

    def forward_weights(j):
        a, b = ys(4 - j), zs(4 - j)
        landed(wg.at[0, a], wrs.at[0, j, 0])
        for i, k in enumerate(NEAR_FIRST):
            go(remote(wg.at[0, a], wg.at[0, a], wss.at[0, 1 + j, i], wrs.at[0, j, k], f, zs(k)))
        landed(wg.at[1, b], wrs.at[1, j, 0])
        for i, k in enumerate(NEAR_FIRST):
            go(remote(wg.at[1, b], wg.at[1, b], wss.at[1, 1 + j, i], wrs.at[1, j, k], f, ys(k)))

    lax.fori_loop(0, 2, fold_rows, 0)
    forward_weights(1)
    forward_weights(3)
    lax.fori_loop(2, 5, fold_rows, 0)
    forward_weights(2)
    lax.fori_loop(5, 10, fold_rows, 0)
    biased = jnp.dot(pbias[...], wc[...], preferred_element_type=F32)
    biased = jnp.sum(biased, axis=0, keepdims=True)
    first = lax.broadcasted_iota(jnp.int32, (128, 512), 0) == 0
    fold[640:768, :] = jnp.where(first, biased, 0.0).astype(BF)
    fold[1408:1536, :] = jnp.zeros((128, 512), BF)
    text_rows(t, f)
    landed(vp, vrs)
    for a in range(2):
        pick = facts[a][0]
        chosen = jnp.zeros((256, 1280), F32)
        for n in range(2):
            chosen = jnp.where(pick == core * 2 + n, v[n].astype(F32), chosen)
            chosen = jnp.where(pick == 2 - core * 2 + n, vp[n].astype(F32), chosen)
        st[a * 256 : a * 256 + 256, :] = chosen.astype(BF)

    def norm_rows(i, carry):
        rows = pl.ds(pl.multiple_of(i * 128, 128), 128)
        x = st[rows, :].astype(F32)
        centred = x - jnp.mean(x, axis=1, keepdims=True)
        spread = jnp.mean(centred * centred, axis=1, keepdims=True)
        nrm[rows, :] = (centred * lax.rsqrt(spread + 1e-6) * ln_g[...] + ln_b[...]).astype(BF)
        return carry

    lax.fori_loop(0, 4, norm_rows, 0)
    for j in NEAR_FIRST:
        fs = xs(4 - j)
        landed(tg.at[fs], trs.at[0, j])
        go(remote(tg.at[fs], tg.at[fs], tss.at[1, j], trs.at[1, j], fp, s))
        text_rows(tg.at[fs], fs)
    for j in (0, 1, 3, 2):
        fs = (f // 2 + 4 - j) % 4 * 2 + 1 - core
        landed(tg.at[fs], trs.at[1, j])
        text_rows(tg.at[fs], fs)
    for j in range(4):
        for k in (1, 2, 3):
            a = ys(4 - j) // 4 * 4 + zs(4 - k) % 4
            b = ys(4 - k) // 4 * 4 + zs(4 - j) % 4
            landed(wg.at[0, a], wrs.at[0, j, k])
            landed(wg.at[1, b], wrs.at[1, j, k])

    def project(i, carry):
        rows = pl.ds(pl.multiple_of(i * 128, 128), 128)
        n = nrm[rows, :]
        both = jnp.dot(n, wg[0].reshape(1280, 1280), preferred_element_type=F32)
        qk[rows, :640] = (both[:, :640] + qkvb[:, lanes(0)]).astype(BF)
        qk[rows, 640:] = (both[:, 640:] + qkvb[:, lanes(1280)]).astype(BF)
        third = jnp.dot(n, wg[1, :, :, :640].reshape(1280, 640), preferred_element_type=F32)
        vv[rows, :] = (third + qkvb[:, lanes(2560)]).astype(BF)
        return carry

    lax.fori_loop(0, 4, project, 0)
    for a in range(2):
        live = lax.broadcasted_iota(jnp.int32, (1, 256), 1) < facts[a][1]
        rows = slice(a * 256, a * 256 + 256)
        for h in range(8):
            q = qk[rows, h * 80 : h * 80 + 80]
            k = qk[rows, 640 + h * 80 : 640 + h * 80 + 80]
            val = vv[rows, h * 80 : h * 80 + 80]
            scores = lax.dot_general(
                q, k, (((1,), (1,)), ((), ())), preferred_element_type=F32
            ) * (1.0 / math.sqrt(80))
            scores = jnp.where(live, scores, NEG)
            weights = jnp.exp(scores - jnp.max(scores, axis=1, keepdims=True))
            prob = (weights / jnp.sum(weights, axis=1, keepdims=True)).astype(BF)
            ctx[rows, h * 80 : h * 80 + 80] = jnp.dot(
                prob, val, preferred_element_type=F32
            ).astype(BF)
    go(remote(ctx, ctxo, ess.at[0], ers.at[0], fp, s))

    def out_rows(owner):
        return wg[1, pl.ds(owner * 8, 8), :, 640:].reshape(640, 640)

    attended = jnp.dot(ctx[...], out_rows(core), preferred_element_type=F32)
    landed(ctxo, ers.at[0])
    attended = attended + jnp.dot(ctxo[...], out_rows(1 - core), preferred_element_type=F32)
    hidden = (st[:, lanes(0)].astype(F32) + attended + outb[:, lanes(0)]).astype(BF)
    quarter = lax.broadcasted_iota(jnp.int32, (128, 512), 1) // 4 == lax.broadcasted_iota(
        jnp.int32, (128, 512), 0
    )
    pooled = jnp.dot(
        jnp.where(quarter, 0.25, 0.0).astype(BF), hidden, preferred_element_type=F32
    )
    pool[...] = pooled.astype(BF)
    go(remote(pool, poolo, ess.at[1], ers.at[1], fp, s))
    landed(poolo, ers.at[1])

    def square(c, total):
        cols = pl.ds(pl.multiple_of(c * 512, 128), 512)
        own_rows = pl.ds(pl.multiple_of(core * 640, 128), 640)
        other_rows = pl.ds(pl.multiple_of(640 - core * 640, 128), 640)
        seen = jnp.dot(pool[...], pw[own_rows, cols], preferred_element_type=F32)
        seen = seen + jnp.dot(poolo[...], pw[other_rows, cols], preferred_element_type=F32)
        seen = seen + pb[:, cols]
        return total + jnp.sum(seen * seen, axis=1, keepdims=True)

    total = lax.fori_loop(0, 8, square, jnp.zeros((128, 1), F32))
    scale = lax.rsqrt(total * (1.0 / 4096) + 1e-5)
    head = (pool[...].astype(F32) * scale).astype(BF)
    tail = jnp.where(lax.broadcasted_iota(jnp.int32, (128, 128), 1) == 0, scale, 0.0).astype(BF)
    want = lax.broadcasted_iota(jnp.int32, (128, 1), 0)
    frame_of = want // 4 % 2
    begin = jnp.where(frame_of == 0, facts[0][2], facts[1][2])
    token = (want // 8 - begin + 16384) % 16 + want % 4 * 16 + frame_of * 64
    taken = (token == lax.broadcasted_iota(jnp.int32, (128, 128), 1)).astype(F32).astype(BF)
    head = jnp.dot(taken, head, preferred_element_type=F32)
    tail = jnp.dot(taken, tail, preferred_element_type=F32)
    for i in range(16):
        tok[i, :, :640] = head[i * 8 : i * 8 + 8].astype(BF)
        tok[i, :, 640:] = tail[i * 8 : i * 8 + 8].astype(BF)
    for k in range(1, 16):
        go(remote(tok.at[seq_at(k)], land.at[s], sss.at[k], srs.at[k], f, seq_at(k)))
    land[s] = tok[s]
    for k in range(1, 16):
        landed(land.at[seq_at(16 - k)], srs.at[k])
    for i, k in enumerate(NEAR_FIRST):
        go(remote(land, table.at[f], xss.at[i], xrs.at[k], xs(k), s))
    go(remote(land, table.at[f], pss.at[0], prs.at[0], fp, s))
    table[f] = land[...]
    for j in NEAR_FIRST:
        fs = xs(4 - j)
        landed(table.at[fs], xrs.at[j])
        go(remote(table.at[fs], table.at[fs], pss.at[j], prs.at[j], fp, s))
    for j in range(4):
        landed(table.at[(f // 2 + 4 - j) % 4 * 2 + 1 - core], prs.at[j])
    parts = []
    for x in range(4):
        even = table[2 * x].astype(F32).reshape(128, 768).astype(BF)
        odd = table[2 * x + 1].astype(F32).reshape(128, 768).astype(BF)
        part = jnp.dot(even, fold[:768, :], preferred_element_type=F32)
        part = part + jnp.dot(odd, fold[768:, :], preferred_element_type=F32)
        parts.append(part.astype(BF))
    visual = jnp.concatenate(parts, axis=0)
    sign = jnp.where(lax.broadcasted_iota(jnp.int32, (1, 128), 1) < 64, -1.0, 1.0)
    factor = math.log2(math.e) / math.sqrt(128)
    for blk in range(4):
        some = slice(blk * 32, blk * 32 + 32)
        shape = (8, 32, 1)
        frame = lax.broadcasted_iota(jnp.int32, shape, 1) + blk * 32
        owner = lax.broadcasted_iota(jnp.int32, shape, 0)
        within = frame * 128 + owner * 16 + s - col[some, 1:2][None]
        live = (within >= 0) & (within < col[some, 2:3][None] // 4)
        source = jnp.where(live, col[some, 0:1][None] + within // 16, -1).reshape(256, 1)
        chosen = (source == lax.broadcasted_iota(jnp.int32, (256, 512), 1)).astype(F32).astype(BF)
        placed = jnp.dot(chosen, visual, preferred_element_type=F32)
        x = jnp.where(source >= 0, placed, plain[blk].reshape(256, 512))
        c1, s1 = ca[some, :][None], sa[some, :][None]
        c2, s2 = cb[...][:, None, :], sb[...][:, None, :]
        cosine = (c1 * c2 - s1 * s2).reshape(256, 128)
        sine = (s1 * c2 + c1 * s2).reshape(256, 128) * sign

        def rotate(n):
            part = x[:, n * 128 : n * 128 + 128]
            return part * cosine + pltpu.roll(part, 64, 1) * sine

        for h in range(2):
            q_out[blk, h * 256 : h * 256 + 256, :] = (rotate(h) * factor).astype(BF)
        rows = slice(blk % 2 * 256, blk % 2 * 256 + 256)
        kv_out[blk // 2, rows, :128] = rotate(2).astype(BF)
        kv_out[blk // 2, rows, 128:] = x[:, 384:].astype(BF)
    for copy in sends:
        copy.wait_send()


def front(rows, vmem_args, hbm_args):
    shape = jax.ShapeDtypeStruct
    dma = pltpu.SemaphoreType.DMA
    vmem = pl.BlockSpec(memory_space=pltpu.VMEM)
    hbm = pl.BlockSpec(memory_space=pl.ANY)
    buf = pltpu.VMEM
    return pl.pallas_call(
        front_kernel,
        out_shape=(shape((4, 512, 128), BF), shape((2, 512, 256), BF)),
        in_specs=[vmem] * (len(rows) + len(vmem_args)) + [hbm] * len(hbm_args),
        out_specs=(vmem, vmem),
        scratch_shapes=[
            buf((2, 80, 1280), BF),
            buf((2, 16, 80, 1280), BF),
            buf((2, 256, 1280), BF),
            buf((8, 128, 4096), BF),
            buf((1280, 4096), BF),
            buf((4096, 512), BF),
            buf((1536, 512), BF),
            buf((4, 8, 32, 512), F32),
            buf((512, 1280), BF),
            buf((512, 1280), BF),
            buf((512, 1280), BF),
            buf((512, 640), BF),
            buf((512, 640), BF),
            buf((512, 640), BF),
            buf((128, 640), BF),
            buf((128, 640), BF),
            buf((16, 8, 768), BF),
            buf((16, 8, 768), BF),
            buf((8, 16, 8, 768), BF),
            buf((128, 128), jnp.int32),
            dma((8,)),
            dma((2, 5, 3)),
            dma((2, 4, 4)),
            dma((2, 4)),
            dma((2, 4)),
            dma,
            dma,
            dma((2,)),
            dma((2,)),
            dma((16,)),
            dma((16,)),
            dma((3,)),
            dma((4,)),
            dma((4,)),
            dma((4,)),
        ],
        compiler_params=pltpu.CompilerParams(
            collective_id=1, has_side_effects=True, vmem_limit_bytes=56 << 20
        ),
        name="front",
    )(*rows, *vmem_args, *hbm_args)


def attend(q_ref, acc, top, den, kv, tile, keys, base, inc):
    scores = lax.dot_general(
        q_ref[tile], kv[:keys, :128], (((1,), (1,)), ((), ())), preferred_element_type=F32
    )
    if base is not None:
        row = lax.broadcasted_iota(jnp.int32, (512, 1), 0) % 256
        col = lax.broadcasted_iota(jnp.int32, (1, keys), 1)
        row = row % 32 * 8 + row // 32 + base + inc
        col = col // 256 * 256 + col % 32 * 8 + col % 256 // 32
        scores = jnp.where(col < row, scores, NEG)
    old = top[tile]
    new = jnp.maximum(old, jnp.max(scores, axis=1, keepdims=True))
    fade = jnp.exp2(old - new)
    weights = jnp.exp2(scores - new[:, :1]).astype(BF)
    top[tile] = new
    wide = jnp.concatenate([kv[:keys, 128:], jnp.ones((keys, 128), BF)], axis=1)
    added = jnp.dot(weights, wide, preferred_element_type=F32)
    den[tile] = den[tile] * fade + added[:, 128:]
    acc[tile] = acc[tile] * fade + added[:, :128]


def by_distance(i):
    return i + i // 2 - i // 3 * 2


def attention_kernel(
    q, own, wo, out, wog, kv, acc, top, den, ctx, local, ss, fs, rs, css, crs, oss, ors
):
    f, s, xs, ys, zs, fp = places()
    y, z = s // 4, s % 4
    greet(
        [(f, ys(k)) for k in (1, 2, 3)]
        + [(f, zs(k)) for k in (1, 2, 3)]
        + [(xs(k), s) for k in (1, 2, 3)]
    )
    sends = []

    def go(copy):
        copy.start()
        sends.append(copy)

    for i, k in enumerate(NEAR_FIRST):
        go(remote(own.at[0], kv.at[0, s], ss.at[0, 0, i], rs.at[0, k, 0], f, ys(k)))
        go(remote(own.at[1], kv.at[1, s], ss.at[1, 0, i], rs.at[1, k, 0], f, zs(k)))
    for i, k in enumerate(NEAR_FIRST):
        go(remote(own.at[0], kv.at[0, s], ss.at[0, 1, i], rs.at[0, 0, k], f, zs(k)))
        go(remote(own.at[1], kv.at[1, s], ss.at[1, 1, i], rs.at[1, 0, k], f, ys(k)))
    for n in range(2):
        go(remote(wo, wog.at[1 + 2 * n], oss.at[n], ors.at[n], xs(3 - 2 * n), s))
    mine = pltpu.make_async_copy(wo, wog.at[0], local.at[1])
    mine.start()
    kv[0, s] = own[0]
    kv[1, s] = own[1]
    top[...] = jnp.full_like(top, NEG)
    den[...] = jnp.zeros_like(den)
    acc[...] = jnp.zeros_like(acc)

    def step(i, carry):
        j = by_distance(jnp.where(i < 4, i, (i - 4) // 3))
        k = by_distance(jnp.where(i < 4, 0, (i - 4) % 3 + 1))
        a = (y + 4 - j) % 4 * 4 + (z + 4 - k) % 4
        b = (y + 4 - k) % 4 * 4 + (z + 4 - j) % 4

        @pl.when(i > 0)
        def _():
            remote(kv.at[0, a], kv.at[0, a], ss.at[0, 0, 0], rs.at[0, j, k], f, s).wait_recv()
            remote(kv.at[1, b], kv.at[1, b], ss.at[0, 0, 0], rs.at[1, j, k], f, s).wait_recv()

        @pl.when((i > 0) & (i < 4))
        def _():
            for n, d in enumerate(NEAR_FIRST):
                remote(
                    kv.at[0, a], kv.at[0, a], fs.at[0, j, n], rs.at[0, j, d], f, zs(d)
                ).start()
                remote(
                    kv.at[1, b], kv.at[1, b], fs.at[1, j, n], rs.at[1, j, d], f, ys(d)
                ).start()

        @pl.when(i == 12)
        def _():
            for n in range(2):
                here = wog.at[1 + 2 * n]
                remote(here, here, oss.at[n], ors.at[n], f, s).wait_recv()
                half = pl.ds(n * 128, 128)
                remote(
                    here.at[half],
                    wog.at[2, half],
                    oss.at[2 + n],
                    ors.at[2 + n],
                    xs(3 - 2 * n),
                    s,
                ).start()

        at = functools.partial(attend, q, acc, top, den)
        inc = jnp.where(a <= s, 1, 0)
        at(kv.at[0, a], 0, 256, 0, inc)
        at(kv.at[0, a], 1, 512, 256, inc)
        at(kv.at[0, a], 2, 512, None, inc)
        at(kv.at[0, a], 3, 512, None, inc)
        inc = jnp.where(b <= s, 1, 0)
        at(kv.at[1, b], 2, 256, 0, inc)
        at(kv.at[1, b], 3, 512, 256, inc)
        return carry

    lax.fori_loop(0, 16, step, 0)
    for tile in range(4):
        block = (acc[tile] / den[tile]).astype(BF)
        for head in range(2):
            for owner in range(8):
                start = head * 256 + owner * 32
                ctx[owner // 2, owner % 2, tile, head] = block[start : start + 32]
    for copy in sends:
        copy.wait_send()

    def drain(j, carry):
        for n in range(3):
            for h in range(2):
                remote(own.at[0], kv.at[0, s], fs.at[h, j, n], rs.at[0, 0, 0], f, s).wait_send()
        return carry

    lax.fori_loop(1, 4, drain, 0)
    x = f // 2
    last = []
    for i, k in enumerate(NEAR_FIRST):
        copy = remote(ctx.at[(x + k) % 4], out.at[4 - k], css.at[i], crs.at[k], xs(k), s)
        copy.start()
        last.append(copy)
    keep = pltpu.make_async_copy(ctx.at[x], out.at[0], local.at[0])
    keep.start()
    for k in (1, 2, 3):
        here = out.at[4 - k]
        remote(here, here, css.at[0], crs.at[k], f, s).wait_recv()
    for copy in last:
        copy.wait_send()
    keep.wait()
    mine.wait()
    for n in range(2):
        half = wog.at[2, pl.ds(n * 128, 128)]
        remote(half, half, oss.at[2 + n], ors.at[2 + n], f, s).wait()


def attention(q, own, wo):
    dma = pltpu.SemaphoreType.DMA
    vmem = pl.BlockSpec(memory_space=pltpu.VMEM)
    hbm = pl.BlockSpec(memory_space=pl.ANY)
    state = pltpu.VMEM((4, 512, 128), F32)
    return pl.pallas_call(
        attention_kernel,
        out_shape=(
            jax.ShapeDtypeStruct((4, 2, 4, 2, 32, 128), BF),
            jax.ShapeDtypeStruct((4, 256, 4096), BF),
        ),
        in_specs=[vmem, vmem, hbm],
        out_specs=(vmem, hbm),
        scratch_shapes=[
            pltpu.VMEM((2, 16, 512, 256), BF),
            state,
            state,
            state,
            pltpu.VMEM((4, 2, 4, 2, 32, 128), BF),
            dma((2,)),
            dma((2, 2, 3)),
            dma((2, 4, 3)),
            dma((2, 4, 4)),
            dma((3,)),
            dma((4,)),
            dma((4,)),
            dma((4,)),
        ],
        compiler_params=pltpu.CompilerParams(
            collective_id=3, has_side_effects=True, vmem_limit_bytes=40 << 20
        ),
        cost_estimate=pl.CostEstimate(
            flops=24_000_000_000, bytes_accessed=9_000_000, transcendentals=20_000_000
        ),
        name="attention",
    )(q, own, wo)


def swap_cores(value):
    return lax.ppermute(value, "frame", [(i, i ^ 1) for i in range(8)])


def per_device(
    vit_states,
    frame_slot,
    patch_count,
    vis_start,
    text_embed,
    vit_ln_gain,
    vit_ln_bias,
    vit_qkv_w,
    vit_qkv_b,
    vit_out_w,
    vit_out_b,
    proj_w,
    proj_b,
    attn_gain,
    wq,
    wk,
    wv,
    wo,
):
    f = lax.axis_index("frame")
    s = lax.axis_index("seq")
    core = f % 2
    text = text_embed.reshape(128, 4096).astype(F32)
    text = (
        text * lax.rsqrt(jnp.mean(text * text, axis=1, keepdims=True) + 1e-5) * attn_gain
    ).astype(BF)
    gained = proj_b * attn_gain
    high = gained.astype(BF)
    low = (gained - high.astype(F32)).astype(BF)
    row = jnp.arange(16)[:, None]
    pbias = jnp.where(row == 0, high[None], jnp.where(row == 1, low[None], jnp.zeros((), BF)))
    exponents = jnp.arange(0, 128, 2).astype(F32) / 128
    inverse = jnp.power(F32(ROPE_THETA), -exponents)
    steps = jnp.concatenate([jnp.arange(128) * 128, jnp.arange(8) * 16 + s]).astype(F32)
    angles = steps[:, None] * jnp.concatenate([inverse, inverse])[None, :]
    cosine, sine = jnp.cos(angles), jnp.sin(angles)
    queries, own = front(
        [frame_slot[None], patch_count[None], vis_start[None]],
        [
            vit_states,
            vit_qkv_w,
            vit_out_w,
            text,
            vit_ln_gain[None],
            vit_ln_bias[None],
            vit_qkv_b[None],
            vit_out_b[None],
            pbias,
            attn_gain[None],
            cosine[:128],
            sine[:128],
            cosine[128:],
            sine[128:],
            proj_b[None],
        ],
        [proj_w, wq, wk, wv],
    )
    ctx, wo_all = attention(queries, own, wo)
    ctx = ctx.transpose(1, 2, 4, 0, 3, 5).reshape(256, 1024)
    partial = jnp.dot(ctx, wo_all.reshape(1024, 4096), preferred_element_type=F32)
    keep = jnp.where(core == 0, partial[:128], partial[128:])
    give = jnp.where(core == 0, partial[128:], partial[:128]).astype(BF)
    mixed = (keep + swap_cores(give).astype(F32)).astype(BF)
    return mixed.reshape(128, 1, 4096)


def solution(mesh):
    return jax.shard_map(
        per_device,
        mesh=mesh,
        in_specs=(
            P(("frame", "seq"), None, None),
            P(),
            P(),
            P(),
            P(None, ("frame", "seq"), None),
            P(),
            P(),
            P("seq", None),
            P(),
            P("seq", None),
            P(),
            P(),
            P(),
            P(),
            P(None, "frame"),
            P(None, "frame"),
            P(None, "frame"),
            P("frame", None),
        ),
        out_specs=P(None, ("frame", "seq"), None),
        check_vma=False,
    )
```

time: 286 us -> 219 us (0.77)
  matrix products: 57.5 us -> 5.72 us
  Pallas kernels: 164 us -> 185 us
  local copies, waits for them, and re-layouts: 33.6 us -> 13.7 us
  starting transfers between devices: 11.8 us -> 0.09 us
  other arithmetic: 10.1 us -> 6.93 us
    dot_general x12 -> x1, matrix products: 57.5 us -> 5.72 us  [per_device(): jnp.dot(ctx, wo_all.reshape(1024, 4096), preferred_element_type=F32)]
    pallas_call x4 -> x2, Pallas kernels: 164 us -> 185 us  [the longest x1 103 us: front(): pl.pallas_call(front_kernel, out_shape=(shape((4, 512, 128), BF), shape((...]
    reshape x4 -> x1, local copies, waits for them, and re-layouts: 9.96 us -> 0.37 us  [per_device(): ctx = ctx.transpose(1, 2, 4, 0, 3, 5).reshape(256, 1024)]
    ppermute x3 -> x1, starting transfers between devices: 8.52 us -> 0.09 us  [swap_cores(): return lax.ppermute(value, 'frame', [(i, i ^ 1) for i in range(8)])]
    unnamed x50 -> x10, local copies, waits for them, and re-layouts: 13.2 us -> 5.31 us
    concatenate x6 -> x0, local copies, waits for them, and re-layouts: 3.85 us -> none  [the longest x1 1.91 us: per_device(): wide = jnp.concatenate([wq, wk, wv], axis=1)]
    ppermute x3 -> x0, starting transfers between devices: 3.25 us -> none  [per_device(): lax.ppermute(wo_late, 'frame', [(i, i ^ k) for i in range(8)])]
  transfers between devices with their start and end apart: 6 -> 1, of which waited for: 2 -> 1; matrix products, arithmetic and copies ran while one was open for 29% -> 0% of each run, Pallas kernels for 38% -> 0%
where the time goes in v2:
time: 219 us; the launch traced here: 215 us
  Pallas kernels  185 us (84%)
  local copies, waits for them, and re-layouts  13.7 us (6%)
  other arithmetic  6.93 us (3%)
  matrix products  5.72 us (3%)
  waiting for transfers between devices  2.65 us (1%)
    pallas_call x1, Pallas kernels, front(): pl.pallas_call(front_kernel, out_shape=(shape((4, 512, 128), BF), shape((...  103 us
    pallas_call x1, Pallas kernels, attention(): pl.pallas_call(attention_kernel, out_shape=(jax.ShapeDtypeStruct((4, 2, 4...  82.7 us
    dot_general x1, matrix products, per_device(): jnp.dot(ctx, wo_all.reshape(1024, 4096), preferred_element_type=F32)  5.72 us
    unnamed x10, local copies, waits for them, and re-layouts  5.31 us
  transfers between devices with their start and end apart: 1, of which 1 were waited for; matrix products, arithmetic and copies ran while one was open for 0% of the time, Pallas kernels for 0%

profile of v2, /device:TPU:1, one launch (start us, length us, event | category | flops | bytes accessed | tf_op | source)
XLA Modules:
  0.0 214.7 jit_solution(13435890468007365355)
XLA Ops:
  0.0 0.0 copy-start.4
  0.0 0.1 pad_maximum_fusion
  0.1 0.3 multiply_sine_fusion
  0.5 0.6 slice.29.sb
  1.1 0.6 slice.27.sa
  1.7 0.6 slice.28.cb
  2.3 0.6 slice.26.ca
  2.9 1.5 fusion
  4.4 1.3 broadcast_in_dim.73.ln_g
  5.7 1.3 broadcast_in_dim.74.ln_b
  7.0 1.3 broadcast_in_dim.76.outb
  8.3 1.3 broadcast_in_dim.75.qkvb
  9.6 0.7 multiply_convert_fusion
  10.4 0.0 copy-done.4
  10.4 2.0 fusion.2.t
  12.4 0.7 select_select_fusion.pbias
  13.1 0.0 copy-start
  13.1 102.7 %front.1 = (bf16[4,512,128]{2,1,0:T(8,128)(2,1)}, bf16[2,512,256]{2,1,0:T(8,128)(2,1)}) custom-call(s32[1,128]{1,0:T(1,128)} %bitcast.19, s32[1,128]{1,0:T(1,128)} %bitcast.20, s32[1,128]{1,0:T(1,128)} %bitcast.21, bf16[2,256,1280]{2,1,0:T(8,128)(2,1)} %v.1, bf16[80,3840]{1,0:T(8,128)(2,1)} %qkvw.1, bf16[80,1280]{1,0:T(8,128)(2,1)} %outw.1, ...), custom_call_target="tpu_custom_call" | custom-call | tf_op jit(solution)/shard_map/front/pallas_call | solution.py:344
  115.9 0.0 copy-done
  115.9 0.0 copy-start.1
  115.9 1.0 copy-done.1
  116.9 0.0 copy-start.2
  116.9 1.0 copy-done.2
  118.0 82.7 %attention.1 = (bf16[4,2,4,2,32,128]{5,4,3,2,1,0:T(8,128)(2,1)S(1)}, bf16[4,256,4096]{2,1,0:T(8,128)(2,1)S(1)}) custom-call(bf16[4,512,128]{2,1,0:T(8,128)(2,1)S(1)} %copy-done.1, bf16[2,512,256]{2,1,0:T(8,128)(2,1)S(1)} %copy-done.2, bf16[256,4096]{1,0:T(8,128)(2,1)S(1)} %copy-done), custom_call_target="tpu_custom_call" | custom-call | flops 24000000000 | bytes 9000000 | tf_op jit(solution)/shard_map/attention/pallas_call | solution.py:539
  200.7 0.0 copy-start.3
  200.7 3.2 %copy-done.3 = bf16[4,256,4096]{2,1,0:T(8,128)(2,1)} copy-done((bf16[4,256,4096]{2,1,0:T(8,128)(2,1)}, bf16[4,256,4096]{2,1,0:T(8,128)(2,1)S(1)}, u32[]{:S(2)}) %copy-start.3) | copy-done | bytes 8388632
  204.0 0.4 copy.19
  204.4 0.4 reshape.47
  204.8 5.7 %fusion.4 = f32[256,4096]{1,0:T(8,128)S(1)} fusion(bf16[256,1024]{1,0:T(8,128)(2,1)S(1)} %reshape.47, bf16[1024,4096]{1,0:T(8,128)(2,1)} %bitcast.16), kind=kOutput, calls=%fused_computation.21 | convolution fusion | flops 2147483648 | bytes 13107200 | tf_op jit(solution)/shard_map/dot_general | solution.py:636
  210.5 0.2 select_convert_fusion
  210.7 0.1 collective-permute-start
  210.8 2.6 %collective-permute-done = bf16[128,4096]{1,0:T(8,128)(2,1)S(1)} collective-permute-done((bf16[128,4096]{1,0:T(8,128)(2,1)S(1)}, bf16[128,4096]{1,0:T(8,128)(2,1)S(1)}, u32[]{:S(2)}, u32[]{:S(2)}) %collective-permute-start) | collective-permute-done | bytes 1048608 | tf_op jit(solution)/shard_map/ppermute | solution.py:573
  213.4 1.3 fusion.3
  (6 shorter events, 0.0 us)
Async XLA Ops:
  0.0 10.4 %copy-start.4 = (bf16[128,1,4096]{2,0,1:T(8,128)(2,1)S(1)}, bf16[128,1,4096]{2,0,1:T(8,128)(2,1)}, u32[]{:S(2)}) copy-start(bf16[128,1,4096]{2,0,1:T(8,128)(2,1)} %param.22) | copy-start | bytes 3145732
  13.1 102.7 %copy-start = (bf16[256,4096]{1,0:T(8,128)(2,1)S(1)}, bf16[256,4096]{1,0:T(8,128)(2,1)}, u32[]{:S(2)}) copy-start(bf16[256,4096]{1,0:T(8,128)(2,1)} %wo.1) | copy-start | bytes 6291460
  115.9 1.0 copy-start.1
  116.9 1.0 copy-start.2
  200.7 3.2 %copy-start.3 = (bf16[4,256,4096]{2,1,0:T(8,128)(2,1)}, bf16[4,256,4096]{2,1,0:T(8,128)(2,1)S(1)}, u32[]{:S(2)}) copy-start(bf16[4,256,4096]{2,1,0:T(8,128)(2,1)S(1)} %get-tuple-element.12) | copy-start | bytes 25165828
  210.7 2.7 %collective-permute-start = (bf16[128,4096]{1,0:T(8,128)(2,1)S(1)}, bf16[128,4096]{1,0:T(8,128)(2,1)S(1)}, u32[]{:S(2)}, u32[]{:S(2)}) collective-permute-start(bf16[128,4096]{1,0:T(8,128)(2,1)S(1)} %select_convert_fusion), channel_id=1, source_target_pairs={{0,16},{16,0},{32,48},{48,32},{64,80},{80,64},{96,112},{112,96},{1... | collective-permute-start | bytes 3145736 | tf_op jit(solution)/shard_map/ppermute | solution.py:573

commit v3 on v2

--- a/solution.py
+++ b/solution.py
@@ -59,11 +59,11 @@
 
 
 def front_kernel(
-    slot_r, count_r, start_r, v, qkvw, outw, t, ln_g, ln_b, qkvb, outb, pbias, again, ca, sa, cb, sb, pb,
-    proj, wq, wk, wv,
-    q_out, kv_out,
+    slot_r, count_r, start_r, v, qkvw, outw, t, vec, trig,
+    proj, wq, wk, wv, wo,
+    q_out, kv_out, wo_half,
     ws, wg, vp, tg, pw, wc, fold, plain, st, nrm, qk, vv, ctx, ctxo, pool, poolo, tok, land, table, col,
-    local, wss, wrs, tss, trs, vss, vrs, ess, ers, sss, srs, xss, xrs, pss, prs,
+    local, wss, wrs, tss, trs, hss, hrs, vss, vrs, ess, ers, sss, srs, xss, xrs, pss, prs, oss, ors,
 ):
     f, s, xs, ys, zs, fp = places()
     core = f % 2
@@ -77,6 +77,8 @@
     def landed(dst, recv):
         remote(dst, dst, vss, recv, fp, s).wait_recv()
 
+    ln_g, ln_b = vec[:, :1280], vec[:, 1280:2560]
+    pb, again = vec[:, 7680:11776], vec[:, 11776:]
     packs = [
         pltpu.make_async_copy(qkvw.at[:, lanes(0)], ws.at[0, :, pl.ds(0, 640)], local.at[0]),
         pltpu.make_async_copy(qkvw.at[:, lanes(1280)], ws.at[0, :, pl.ds(640, 640)], local.at[1]),
@@ -104,16 +106,49 @@
         copy.start()
         sends.append(copy)
 
-    for i, k in enumerate(NEAR_FIRST):
-        go(remote(ws.at[0], wg.at[0, s], wss.at[0, 0, i], wrs.at[0, k, 0], f, ys(k)))
-        go(remote(ws.at[1], wg.at[1, s], wss.at[1, 0, i], wrs.at[1, k, 0], f, zs(k)))
+    def weight_slot(h, j, k):
+        a, b = (4 - j) % 4, (4 - k) % 4
+        if h == 0:
+            return wg.at[0, ys(a) // 4 * 4 + zs(b) % 4]
+        return wg.at[1, ys(b) // 4 * 4 + zs(a) % 4]
+
+    def weight_half(ref, n):
+        return ref.at[:, pl.ds(n * 640, 640)]
+
+    def send_weights(j, k):
+        for h in range(2):
+            first, second = (ys, zs) if h == 0 else (zs, ys)
+            slot = weight_slot(h, j, k)
+            full = ws.at[h] if j == k == 0 else slot
+            plan = []
+            if j == k == 0:
+                plan += [(full, slot, (1, 0, 0), first(1)), (full, slot, (3, 0, 0), first(3))]
+            if k == 0 and j in (1, 3):
+                part = weight_half(slot, j // 2)
+                plan += [(part, part, (2, 0, j // 2), first(j))]
+            if k == 0:
+                plan += [(full, slot, (j, 1, 0), second(1)), (full, slot, (j, 3, 0), second(3))]
+            if k in (1, 3):
+                part = weight_half(slot, k // 2)
+                plan += [(part, part, (j, 2, k // 2), second(k))]
+            for n, (a, b, (jj, kk, m), to) in enumerate(plan):
+                go(remote(a, b, wss.at[h, j, k, n], wrs.at[h, jj, kk, m], f, to))
+
+    def take_weights(j, k):
+        for h in range(2):
+            slot = weight_slot(h, j, k)
+            if k == 2 or (j == 2 and k == 0):
+                landed(weight_half(slot, 0), wrs.at[h, j, k, 0])
+                landed(weight_half(slot, 1), wrs.at[h, j, k, 1])
+            else:
+                landed(slot, wrs.at[h, j, k, 0])
+        send_weights(j, k)
+
+    send_weights(0, 0)
     go(remote(v, vp, vss, vrs, fp, s))
-    for i, k in enumerate(NEAR_FIRST):
-        go(remote(t, tg.at[f], tss.at[0, i], trs.at[0, k], xs(k), s))
-    go(remote(t, tg.at[f], tss.at[1, 0], trs.at[1, 0], fp, s))
-    for i, k in enumerate(NEAR_FIRST):
-        go(remote(ws.at[0], wg.at[0, s], wss.at[0, 1, i], wrs.at[0, 0, k], f, zs(k)))
-        go(remote(ws.at[1], wg.at[1, s], wss.at[1, 1, i], wrs.at[1, 0, k], f, ys(k)))
+    go(remote(t, tg.at[f], tss.at[0], trs.at[1], xs(1), s))
+    go(remote(t, tg.at[f], tss.at[1], trs.at[3], xs(3), s))
+    go(remote(t, tg.at[f], hss.at[0, 0], hrs.at[0, 0], fp, s))
     for copy in loads:
         copy.start()
     wg[0, s] = ws[0]
@@ -150,29 +185,34 @@
     def fold_rows(i, carry):
         rows = pl.ds(pl.multiple_of(i * 128, 128), 128)
         to = pl.ds(pl.multiple_of(i * 128 + i // 5 * 128, 128), 128)
-        gained = (pw[rows, :].astype(F32) * again[...]).astype(BF)
+        gained = (pw[rows, :].astype(F32) * again).astype(BF)
         fold[to, :] = jnp.dot(gained, wc[...], preferred_element_type=F32).astype(BF)
         return carry
 
     def text_rows(source, at):
         plain[:, at] = jnp.dot(source[...], wc[...], preferred_element_type=F32).reshape(4, 32, 512)
 
-    def forward_weights(j):
-        a, b = ys(4 - j), zs(4 - j)
-        landed(wg.at[0, a], wrs.at[0, j, 0])
-        for i, k in enumerate(NEAR_FIRST):
-            go(remote(wg.at[0, a], wg.at[0, a], wss.at[0, 1 + j, i], wrs.at[0, j, k], f, zs(k)))
-        landed(wg.at[1, b], wrs.at[1, j, 0])
-        for i, k in enumerate(NEAR_FIRST):
-            go(remote(wg.at[1, b], wg.at[1, b], wss.at[1, 1 + j, i], wrs.at[1, j, k], f, ys(k)))
-
-    lax.fori_loop(0, 2, fold_rows, 0)
-    forward_weights(1)
-    forward_weights(3)
-    lax.fori_loop(2, 5, fold_rows, 0)
-    forward_weights(2)
-    lax.fori_loop(5, 10, fold_rows, 0)
-    biased = jnp.dot(pbias[...], wc[...], preferred_element_type=F32)
+    def text_half(ref, n):
+        return ref.at[pl.ds(n * 64, 64)]
+
+    lax.fori_loop(0, 3, fold_rows, 0)
+    take_weights(1, 0)
+    take_weights(3, 0)
+    lax.fori_loop(3, 6, fold_rows, 0)
+    take_weights(0, 1)
+    take_weights(0, 3)
+    take_weights(2, 0)
+    lax.fori_loop(6, 8, fold_rows, 0)
+    take_weights(1, 1)
+    take_weights(1, 3)
+    lax.fori_loop(8, 10, fold_rows, 0)
+    take_weights(3, 1)
+    take_weights(3, 3)
+    row = lax.broadcasted_iota(jnp.int32, (16, 1), 0)
+    biased = pb * again
+    upper = biased.astype(BF).astype(F32)
+    biased = jnp.where(row == 0, upper, jnp.where(row == 1, biased - upper, 0.0)).astype(BF)
+    biased = jnp.dot(biased, wc[...], preferred_element_type=F32)
     biased = jnp.sum(biased, axis=0, keepdims=True)
     first = lax.broadcasted_iota(jnp.int32, (128, 512), 0) == 0
     fold[640:768, :] = jnp.where(first, biased, 0.0).astype(BF)
@@ -192,34 +232,53 @@
         x = st[rows, :].astype(F32)
         centred = x - jnp.mean(x, axis=1, keepdims=True)
         spread = jnp.mean(centred * centred, axis=1, keepdims=True)
-        nrm[rows, :] = (centred * lax.rsqrt(spread + 1e-6) * ln_g[...] + ln_b[...]).astype(BF)
+        nrm[rows, :] = (centred * lax.rsqrt(spread + 1e-6) * ln_g + ln_b).astype(BF)
         return carry
 
     lax.fori_loop(0, 4, norm_rows, 0)
-    for j in NEAR_FIRST:
+    take_weights(2, 1)
+    take_weights(2, 3)
+    for j in (1, 3):
         fs = xs(4 - j)
-        landed(tg.at[fs], trs.at[0, j])
-        go(remote(tg.at[fs], tg.at[fs], tss.at[1, j], trs.at[1, j], fp, s))
+        here = tg.at[fs]
+        landed(here, trs.at[j])
+        part = text_half(here, j // 2)
+        go(remote(part, part, tss.at[2 + j // 2], hrs.at[2, j // 2], xs(j), s))
+        go(remote(here, here, hss.at[1, j // 2], hrs.at[1, j // 2], fp, s))
+    for n in range(2):
+        half = pl.ds(n * 128, 128)
+        go(remote(wo.at[half], wo_half.at[n], oss.at[n], ors.at[n], xs(1 + 2 * n), s))
+    for j in (1, 3):
+        text_rows(tg.at[xs(4 - j)], xs(4 - j))
+    landed(tg.at[fp], hrs.at[0, 0])
+    text_rows(tg.at[fp], fp)
+    take_weights(0, 2)
+    for j in (1, 3):
+        fs = xs(4 - j) + 1 - 2 * core
+        landed(tg.at[fs], hrs.at[1, j // 2])
         text_rows(tg.at[fs], fs)
-    for j in (0, 1, 3, 2):
-        fs = (f // 2 + 4 - j) % 4 * 2 + 1 - core
-        landed(tg.at[fs], trs.at[1, j])
-        text_rows(tg.at[fs], fs)
-    for j in range(4):
-        for k in (1, 2, 3):
-            a = ys(4 - j) // 4 * 4 + zs(4 - k) % 4
-            b = ys(4 - k) // 4 * 4 + zs(4 - j) % 4
-            landed(wg.at[0, a], wrs.at[0, j, k])
-            landed(wg.at[1, b], wrs.at[1, j, k])
+    take_weights(1, 2)
+    take_weights(3, 2)
+    far = xs(2)
+    for n in range(2):
+        part = text_half(tg.at[far], n)
+        landed(part, hrs.at[2, n])
+        go(remote(part, part, hss.at[2, n], hrs.at[3, n], fp, s))
+    text_rows(tg.at[far], far)
+    far = far + 1 - 2 * core
+    for n in range(2):
+        landed(text_half(tg.at[far], n), hrs.at[3, n])
+    text_rows(tg.at[far], far)
+    take_weights(2, 2)
 
     def project(i, carry):
         rows = pl.ds(pl.multiple_of(i * 128, 128), 128)
         n = nrm[rows, :]
         both = jnp.dot(n, wg[0].reshape(1280, 1280), preferred_element_type=F32)
-        qk[rows, :640] = (both[:, :640] + qkvb[:, lanes(0)]).astype(BF)
-        qk[rows, 640:] = (both[:, 640:] + qkvb[:, lanes(1280)]).astype(BF)
+        qk[rows, :640] = (both[:, :640] + vec[:, lanes(3840)]).astype(BF)
+        qk[rows, 640:] = (both[:, 640:] + vec[:, lanes(5120)]).astype(BF)
         third = jnp.dot(n, wg[1, :, :, :640].reshape(1280, 640), preferred_element_type=F32)
-        vv[rows, :] = (third + qkvb[:, lanes(2560)]).astype(BF)
+        vv[rows, :] = (third + vec[:, lanes(6400)]).astype(BF)
         return carry
 
     lax.fori_loop(0, 4, project, 0)
@@ -247,7 +306,7 @@
     attended = jnp.dot(ctx[...], out_rows(core), preferred_element_type=F32)
     landed(ctxo, ers.at[0])
     attended = attended + jnp.dot(ctxo[...], out_rows(1 - core), preferred_element_type=F32)
-    hidden = (st[:, lanes(0)].astype(F32) + attended + outb[:, lanes(0)]).astype(BF)
+    hidden = (st[:, lanes(0)].astype(F32) + attended + vec[:, lanes(2560)]).astype(BF)
     quarter = lax.broadcasted_iota(jnp.int32, (128, 512), 1) // 4 == lax.broadcasted_iota(
         jnp.int32, (128, 512), 0
     )
@@ -264,7 +323,7 @@
         other_rows = pl.ds(pl.multiple_of(640 - core * 640, 128), 640)
         seen = jnp.dot(pool[...], pw[own_rows, cols], preferred_element_type=F32)
         seen = seen + jnp.dot(poolo[...], pw[other_rows, cols], preferred_element_type=F32)
-        seen = seen + pb[:, cols]
+        seen = seen + vec[:, pl.ds(pl.multiple_of(7680 + c * 512, 128), 512)]
         return total + jnp.sum(seen * seen, axis=1, keepdims=True)
 
     total = lax.fori_loop(0, 8, square, jnp.zeros((128, 1), F32))
@@ -317,8 +376,8 @@
         chosen = (source == lax.broadcasted_iota(jnp.int32, (256, 512), 1)).astype(F32).astype(BF)
         placed = jnp.dot(chosen, visual, preferred_element_type=F32)
         x = jnp.where(source >= 0, placed, plain[blk].reshape(256, 512))
-        c1, s1 = ca[some, :][None], sa[some, :][None]
-        c2, s2 = cb[...][:, None, :], sb[...][:, None, :]
+        c1, s1 = trig[0, some, :][None], trig[1, some, :][None]
+        c2, s2 = trig[0, 128:, :][:, None, :], trig[1, 128:, :][:, None, :]
         cosine = (c1 * c2 - s1 * s2).reshape(256, 128)
         sine = (s1 * c2 + c1 * s2).reshape(256, 128) * sign
 
@@ -331,6 +390,8 @@
         rows = slice(blk % 2 * 256, blk % 2 * 256 + 256)
         kv_out[blk // 2, rows, :128] = rotate(2).astype(BF)
         kv_out[blk // 2, rows, 128:] = x[:, 384:].astype(BF)
+    for n in range(2):
+        landed(wo_half.at[n], ors.at[n])
     for copy in sends:
         copy.wait_send()
 
@@ -343,9 +404,13 @@
     buf = pltpu.VMEM
     return pl.pallas_call(
         front_kernel,
-        out_shape=(shape((4, 512, 128), BF), shape((2, 512, 256), BF)),
+        out_shape=(
+            shape((4, 512, 128), BF),
+            shape((2, 512, 256), BF),
+            shape((2, 128, 4096), BF),
+        ),
         in_specs=[vmem] * (len(rows) + len(vmem_args)) + [hbm] * len(hbm_args),
-        out_specs=(vmem, vmem),
+        out_specs=(vmem, vmem, hbm),
         scratch_shapes=[
             buf((2, 80, 1280), BF),
             buf((2, 16, 80, 1280), BF),
@@ -368,10 +433,12 @@
             buf((8, 16, 8, 768), BF),
             buf((128, 128), jnp.int32),
             dma((8,)),
-            dma((2, 5, 3)),
-            dma((2, 4, 4)),
-            dma((2, 4)),
-            dma((2, 4)),
+            dma((2, 4, 4, 4)),
+            dma((2, 4, 4, 2)),
+            dma((4,)),
+            dma((4,)),
+            dma((3, 2)),
+            dma((4, 2)),
             dma,
             dma,
             dma((2,)),
@@ -382,6 +449,8 @@
             dma((4,)),
             dma((4,)),
             dma((4,)),
+            dma((2,)),
+            dma((2,)),
         ],
         compiler_params=pltpu.CompilerParams(
             collective_id=1, has_side_effects=True, vmem_limit_bytes=56 << 20
@@ -411,36 +480,83 @@
     acc[tile] = acc[tile] * fade + added[:, :128]
 
 
-def by_distance(i):
-    return i + i // 2 - i // 3 * 2
+ORDER = (
+    (0, 0), (1, 0), (3, 0), (0, 1), (0, 3), (2, 0), (1, 1), (1, 3),
+    (3, 1), (3, 3), (0, 2), (2, 1), (2, 3), (1, 2), (3, 2), (2, 2),
+)
 
 
 def attention_kernel(
-    q, own, wo, out, wog, kv, acc, top, den, ctx, local, ss, fs, rs, css, crs, oss, ors
+    q, own, wo, wo_half, out, kv, acc, top, den, ctx, seen, lhs, wog, give, got,
+    local, ss, rs, css, crs, oss, ors, gss, grs,
 ):
     f, s, xs, ys, zs, fp = places()
+    core = f % 2
     y, z = s // 4, s % 4
     greet(
-        [(f, ys(k)) for k in (1, 2, 3)]
-        + [(f, zs(k)) for k in (1, 2, 3)]
+        [(f, ys(1)), (f, ys(3)), (f, zs(1)), (f, zs(3))]
         + [(xs(k), s) for k in (1, 2, 3)]
-    )
-    sends = []
-
-    def go(copy):
+        + [(fp, s)]
+    )
+
+    def slot_of(h, j, k):
+        a, b = (4 - j) % 4, (4 - k) % 4
+        if h == 0:
+            return kv.at[0, ys(a) // 4 * 4 + zs(b) % 4]
+        return kv.at[1, ys(b) // 4 * 4 + zs(a) % 4]
+
+    def half_of(ref, n):
+        return ref.at[pl.ds(n * 256, 256)]
+
+    def copies_of(j, k):
+        result = []
+        for h in range(2):
+            first, second = (ys, zs) if h == 0 else (zs, ys)
+            slot = slot_of(h, j, k)
+            full = own.at[h] if j == k == 0 else slot
+            plan = []
+            if j == k == 0:
+                plan += [(full, slot, (1, 0, 0), first(1)), (full, slot, (3, 0, 0), first(3))]
+            if k == 0 and j in (1, 3):
+                part = half_of(slot, j // 2)
+                plan += [(part, part, (2, 0, j // 2), first(j))]
+            if k == 0:
+                plan += [(full, slot, (j, 1, 0), second(1)), (full, slot, (j, 3, 0), second(3))]
+            if k in (1, 3):
+                part = half_of(slot, k // 2)
+                plan += [(part, part, (j, 2, k // 2), second(k))]
+            for n, (a, b, (jj, kk, m), to) in enumerate(plan):
+                result.append(remote(a, b, ss.at[h, j, k, n], rs.at[h, jj, kk, m], f, to))
+        return result
+
+    def landed(dst, recv):
+        remote(dst, dst, local.at[0], recv, fp, s).wait_recv()
+
+    def take(j, k):
+        for h in range(2):
+            slot = slot_of(h, j, k)
+            if k == 2 or (j == 2 and k == 0):
+                landed(half_of(slot, 0), rs.at[h, j, k, 0])
+                landed(half_of(slot, 1), rs.at[h, j, k, 1])
+            else:
+                landed(slot, rs.at[h, j, k, 0])
+
+    for copy in copies_of(0, 0):
         copy.start()
-        sends.append(copy)
-
-    for i, k in enumerate(NEAR_FIRST):
-        go(remote(own.at[0], kv.at[0, s], ss.at[0, 0, i], rs.at[0, k, 0], f, ys(k)))
-        go(remote(own.at[1], kv.at[1, s], ss.at[1, 0, i], rs.at[1, k, 0], f, zs(k)))
-    for i, k in enumerate(NEAR_FIRST):
-        go(remote(own.at[0], kv.at[0, s], ss.at[0, 1, i], rs.at[0, 0, k], f, zs(k)))
-        go(remote(own.at[1], kv.at[1, s], ss.at[1, 1, i], rs.at[1, 0, k], f, ys(k)))
-    for n in range(2):
-        go(remote(wo, wog.at[1 + 2 * n], oss.at[n], ors.at[n], xs(3 - 2 * n), s))
-    mine = pltpu.make_async_copy(wo, wog.at[0], local.at[1])
-    mine.start()
+    lower, upper = pl.ds(0, 128), pl.ds(128, 128)
+    parts = [
+        remote(wo_half.at[0], wog.at[2, lower], oss.at[0], ors.at[0], xs(1), s),
+        remote(wo_half.at[1], wog.at[2, upper], oss.at[1], ors.at[1], xs(3), s),
+        remote(wo.at[upper], wog.at[3, upper], oss.at[2], ors.at[2], xs(1), s),
+        remote(wo.at[lower], wog.at[1, lower], oss.at[3], ors.at[3], xs(3), s),
+    ]
+    keeps = [
+        pltpu.make_async_copy(wo, wog.at[0], local.at[1]),
+        pltpu.make_async_copy(wo_half.at[0], wog.at[3, lower], local.at[2]),
+        pltpu.make_async_copy(wo_half.at[1], wog.at[1, upper], local.at[3]),
+    ]
+    for copy in parts + keeps:
+        copy.start()
     kv[0, s] = own[0]
     kv[1, s] = own[1]
     top[...] = jnp.full_like(top, NEG)
@@ -448,41 +564,20 @@
     acc[...] = jnp.zeros_like(acc)
 
     def step(i, carry):
-        j = by_distance(jnp.where(i < 4, i, (i - 4) // 3))
-        k = by_distance(jnp.where(i < 4, 0, (i - 4) % 3 + 1))
+        j = k = 0
+        for n, (jj, kk) in enumerate(ORDER):
+            if n > 0:
+                j = jnp.where(i == n, jj, j)
+                k = jnp.where(i == n, kk, k)
+
+                @pl.when(i == n)
+                def _(jj=jj, kk=kk):
+                    take(jj, kk)
+                    for copy in copies_of(jj, kk):
+                        copy.start()
+
         a = (y + 4 - j) % 4 * 4 + (z + 4 - k) % 4
         b = (y + 4 - k) % 4 * 4 + (z + 4 - j) % 4
-
-        @pl.when(i > 0)
-        def _():
-            remote(kv.at[0, a], kv.at[0, a], ss.at[0, 0, 0], rs.at[0, j, k], f, s).wait_recv()
-            remote(kv.at[1, b], kv.at[1, b], ss.at[0, 0, 0], rs.at[1, j, k], f, s).wait_recv()
-
-        @pl.when((i > 0) & (i < 4))
-        def _():
-            for n, d in enumerate(NEAR_FIRST):
-                remote(
-                    kv.at[0, a], kv.at[0, a], fs.at[0, j, n], rs.at[0, j, d], f, zs(d)
-                ).start()
-                remote(
-                    kv.at[1, b], kv.at[1, b], fs.at[1, j, n], rs.at[1, j, d], f, ys(d)
-                ).start()
-
-        @pl.when(i == 12)
-        def _():
-            for n in range(2):
-                here = wog.at[1 + 2 * n]
-                remote(here, here, oss.at[n], ors.at[n], f, s).wait_recv()
-                half = pl.ds(n * 128, 128)
-                remote(
-                    here.at[half],
-                    wog.at[2, half],
-                    oss.at[2 + n],
-                    ors.at[2 + n],
-                    xs(3 - 2 * n),
-                    s,
-                ).start()
-
         at = functools.partial(attend, q, acc, top, den)
         inc = jnp.where(a <= s, 1, 0)
         at(kv.at[0, a], 0, 256, 0, inc)
@@ -501,76 +596,103 @@
             for owner in range(8):
                 start = head * 256 + owner * 32
                 ctx[owner // 2, owner % 2, tile, head] = block[start : start + 32]
-    for copy in sends:
-        copy.wait_send()
-
-    def drain(j, carry):
-        for n in range(3):
-            for h in range(2):
-                remote(own.at[0], kv.at[0, s], fs.at[h, j, n], rs.at[0, 0, 0], f, s).wait_send()
-        return carry
-
-    lax.fori_loop(1, 4, drain, 0)
+    for j, k in ORDER:
+        for copy in copies_of(j, k):
+            copy.wait_send()
     x = f // 2
     last = []
     for i, k in enumerate(NEAR_FIRST):
-        copy = remote(ctx.at[(x + k) % 4], out.at[4 - k], css.at[i], crs.at[k], xs(k), s)
+        last.append(remote(ctx.at[(x + k) % 4], seen.at[4 - k], css.at[i], crs.at[k], xs(k), s))
+    for copy in last:
         copy.start()
-        last.append(copy)
-    keep = pltpu.make_async_copy(ctx.at[x], out.at[0], local.at[0])
-    keep.start()
-    for k in (1, 2, 3):
-        here = out.at[4 - k]
-        remote(here, here, css.at[0], crs.at[k], f, s).wait_recv()
+    seen[0] = ctx[x]
+    for copy in keeps:
+        copy.wait()
+    for copy in parts:
+        copy.wait()
+    for k in (1, 3, 2):
+        landed(seen.at[4 - k], crs.at[k])
+    for d in range(4):
+        for head in range(2):
+            cols = slice(d * 256 + head * 128, d * 256 + head * 128 + 128)
+            for owner in range(2):
+                lhs[owner, :, cols] = seen[d, owner, :, head].reshape(128, 128)
+
+    def columns(c):
+        return pl.ds(pl.multiple_of(c * 512, 128), 512)
+
+    def share(c):
+        return remote(
+            give.at[:, columns(c)], got.at[:, columns(c)], gss.at[c], grs.at[c], fp, s
+        )
+
+    def partial(owner, c):
+        return jnp.dot(
+            lhs[owner], wog[:, :, columns(c)].reshape(1024, 512), preferred_element_type=F32
+        )
+
+    def to_partner(c, carry):
+        give[:, columns(c)] = partial(1 - core, c).astype(BF)
+
+        @pl.when(c > 0)
+        def _():
+            share(c - 1).start()
+
+        return carry
+
+    def to_output(c, carry):
+        mine = partial(core, c)
+
+        @pl.when(c == 0)
+        def _():
+            share(7).start()
+
+        share(c).wait()
+        out[:, columns(c)] = (mine + got[:, columns(c)].astype(F32)).astype(BF)
+        return carry
+
+    lax.fori_loop(0, 8, to_partner, 0)
+    lax.fori_loop(0, 8, to_output, 0)
     for copy in last:
         copy.wait_send()
-    keep.wait()
-    mine.wait()
-    for n in range(2):
-        half = wog.at[2, pl.ds(n * 128, 128)]
-        remote(half, half, oss.at[2 + n], ors.at[2 + n], f, s).wait()
-
-
-def attention(q, own, wo):
+
+
+def attention(q, own, wo, wo_half):
     dma = pltpu.SemaphoreType.DMA
     vmem = pl.BlockSpec(memory_space=pltpu.VMEM)
     hbm = pl.BlockSpec(memory_space=pl.ANY)
     state = pltpu.VMEM((4, 512, 128), F32)
     return pl.pallas_call(
         attention_kernel,
-        out_shape=(
-            jax.ShapeDtypeStruct((4, 2, 4, 2, 32, 128), BF),
-            jax.ShapeDtypeStruct((4, 256, 4096), BF),
-        ),
-        in_specs=[vmem, vmem, hbm],
-        out_specs=(vmem, hbm),
+        out_shape=jax.ShapeDtypeStruct((128, 4096), BF),
+        in_specs=[vmem, vmem, hbm, hbm],
+        out_specs=vmem,
         scratch_shapes=[
             pltpu.VMEM((2, 16, 512, 256), BF),
             state,
             state,
             state,
             pltpu.VMEM((4, 2, 4, 2, 32, 128), BF),
-            dma((2,)),
-            dma((2, 2, 3)),
-            dma((2, 4, 3)),
-            dma((2, 4, 4)),
+            pltpu.VMEM((4, 2, 4, 2, 32, 128), BF),
+            pltpu.VMEM((2, 128, 1024), BF),
+            pltpu.VMEM((4, 256, 4096), BF),
+            pltpu.VMEM((128, 4096), BF),
+            pltpu.VMEM((128, 4096), BF),
+            dma((4,)),
+            dma((2, 4, 4, 4)),
+            dma((2, 4, 4, 2)),
             dma((3,)),
             dma((4,)),
             dma((4,)),
             dma((4,)),
+            dma((8,)),
+            dma((8,)),
         ],
         compiler_params=pltpu.CompilerParams(
-            collective_id=3, has_side_effects=True, vmem_limit_bytes=40 << 20
-        ),
-        cost_estimate=pl.CostEstimate(
-            flops=24_000_000_000, bytes_accessed=9_000_000, transcendentals=20_000_000
+            collective_id=3, has_side_effects=True, vmem_limit_bytes=48 << 20
         ),
         name="attention",
-    )(q, own, wo)
-
-
-def swap_cores(value):
-    return lax.ppermute(value, "frame", [(i, i ^ 1) for i in range(8)])
+    )(q, own, wo, wo_half)
 
 
 def per_device(
@@ -593,51 +715,23 @@
     wv,
     wo,
 ):
-    f = lax.axis_index("frame")
     s = lax.axis_index("seq")
-    core = f % 2
     text = text_embed.reshape(128, 4096).astype(F32)
     text = (
         text * lax.rsqrt(jnp.mean(text * text, axis=1, keepdims=True) + 1e-5) * attn_gain
     ).astype(BF)
-    gained = proj_b * attn_gain
-    high = gained.astype(BF)
-    low = (gained - high.astype(F32)).astype(BF)
-    row = jnp.arange(16)[:, None]
-    pbias = jnp.where(row == 0, high[None], jnp.where(row == 1, low[None], jnp.zeros((), BF)))
     exponents = jnp.arange(0, 128, 2).astype(F32) / 128
     inverse = jnp.power(F32(ROPE_THETA), -exponents)
     steps = jnp.concatenate([jnp.arange(128) * 128, jnp.arange(8) * 16 + s]).astype(F32)
     angles = steps[:, None] * jnp.concatenate([inverse, inverse])[None, :]
-    cosine, sine = jnp.cos(angles), jnp.sin(angles)
-    queries, own = front(
+    trig = jnp.stack([jnp.cos(angles), jnp.sin(angles)])
+    vectors = [vit_ln_gain, vit_ln_bias, vit_out_b, vit_qkv_b, proj_b, attn_gain]
+    queries, own, wo_half = front(
         [frame_slot[None], patch_count[None], vis_start[None]],
-        [
-            vit_states,
-            vit_qkv_w,
-            vit_out_w,
-            text,
-            vit_ln_gain[None],
-            vit_ln_bias[None],
-            vit_qkv_b[None],
-            vit_out_b[None],
-            pbias,
-            attn_gain[None],
-            cosine[:128],
-            sine[:128],
-            cosine[128:],
-            sine[128:],
-            proj_b[None],
-        ],
-        [proj_w, wq, wk, wv],
-    )
-    ctx, wo_all = attention(queries, own, wo)
-    ctx = ctx.transpose(1, 2, 4, 0, 3, 5).reshape(256, 1024)
-    partial = jnp.dot(ctx, wo_all.reshape(1024, 4096), preferred_element_type=F32)
-    keep = jnp.where(core == 0, partial[:128], partial[128:])
-    give = jnp.where(core == 0, partial[128:], partial[:128]).astype(BF)
-    mixed = (keep + swap_cores(give).astype(F32)).astype(BF)
-    return mixed.reshape(128, 1, 4096)
+        [vit_states, vit_qkv_w, vit_out_w, text, jnp.concatenate(vectors)[None], trig],
+        [proj_w, wq, wk, wv, wo],
+    )
+    return attention(queries, own, wo, wo_half).reshape(128, 1, 4096)
 
 
 def solution(mesh):

time: 219 us -> 198 us (0.904); the launches traced: 215 us -> 197 us
  matrix products: 5.72 us -> 0 us
  local copies, waits for them, and re-layouts: 13.7 us -> 8.01 us
  waiting for transfers between devices: 2.65 us -> 0 us
  other arithmetic: 6.93 us -> 4.71 us
    dot_general x1 -> x0, matrix products: 5.72 us -> none  [per_device(): jnp.dot(ctx, wo_all.reshape(1024, 4096), preferred_element_type=F32)]
    broadcast_in_dim x4 -> x1, local copies, waits for them, and re-layouts: 5.2 us -> 0.67 us  [per_device(): jnp.concatenate(vectors)[None]]
    ppermute x1 -> x0, waiting for transfers between devices: 2.65 us -> none  [swap_cores(): return lax.ppermute(value, 'frame', [(i, i ^ 1) for i in range(8)])]
    slice x4 -> x0, local copies, waits for them, and re-layouts: 2.44 us -> none  [the longest x1 0.63 us: per_device(): sine[:128]]
    unnamed x10 -> x14, local copies, waits for them, and re-layouts: 5.31 us -> 6.62 us
  transfers between devices with their start and end apart: 1 -> 0, of which waited for: 1 -> 0; matrix products, arithmetic and copies ran while one was open for 0% -> 0% of each run, Pallas kernels for 0% -> 0%
where the time goes in v3:
time: 198 us; the launch traced here: 197 us
  Pallas kernels  184 us (93%)
  local copies, waits for them, and re-layouts  8.01 us (4%)
  other arithmetic  4.71 us (2%)
    pallas_call x1, Pallas kernels, front(): pl.pallas_call(front_kernel, out_shape=(shape((4, 512, 128), BF), shape((...  102 us
    pallas_call x1, Pallas kernels, attention(): pl.pallas_call(attention_kernel, out_shape=jax.ShapeDtypeStruct((128, 409...  82 us
    unnamed x14, local copies, waits for them, and re-layouts  6.62 us

profile of v3, /device:TPU:1, one launch (start us, length us, event | category | flops | bytes accessed | tf_op | source)
XLA Modules:
  0.0 197.1 jit_solution(4749803196948907126)
XLA Ops:
  0.0 0.0 copy-start.3
  0.0 1.6 fusion
  1.7 0.1 pad_maximum_fusion.1
  1.7 0.7 constant_dynamic-update-slice_fusion.5
  2.4 0.7 constant_dynamic-update-slice_fusion.4
  3.1 0.7 constant_dynamic-update-slice_fusion.3
  3.9 0.7 constant_dynamic-update-slice_fusion.2
  4.6 0.7 constant_dynamic-update-slice_fusion.1
  5.3 0.7 constant_dynamic-update-slice_fusion
  6.0 0.7 broadcast_in_dim.19.vec
  6.7 0.3 multiply_cosine_fusion
  7.0 0.7 pad_maximum_fusion.trig
  7.7 0.0 copy-done.3
  7.7 2.0 %fusion.2.t = bf16[128,4096]{1,0:T(8,128)(2,1)} fusion(bf16[128,1,4096]{2,0,1:T(8,128)(2,1)S(1)} %copy-done.3, f32[4096]{0:T(1024)} %param.31, f32[128]{0:T(128)S(1)} %add_rsqrt_fusion), kind=kLoop, calls=%fused_computation.4 | loop fusion | flops 2097152 | bytes 2114048 | tf_op jit(solution)/shard_map/convert_element_type | solution.py:722
  9.7 0.0 copy-start
  9.7 102.3 %front.1 = (bf16[4,512,128]{2,1,0:T(8,128)(2,1)}, bf16[2,512,256]{2,1,0:T(8,128)(2,1)}, bf16[2,128,4096]{2,1,0:T(8,128)(2,1)}) custom-call(s32[1,128]{1,0:T(1,128)} %bitcast.9, s32[1,128]{1,0:T(1,128)} %bitcast.10, s32[1,128]{1,0:T(1,128)} %bitcast.11, bf16[2,256,1280]{2,1,0:T(8,128)(2,1)} %v.1, bf16[80,3840]{1,0:T(8,128)(2,1)} %qkvw.1, ...), custom_call_target="tpu_custom_call" | custom-call | tf_op jit(solution)/shard_map/front/pallas_call | solution.py:405
  112.0 0.0 copy-done
  112.0 0.0 copy-start.1
  112.1 1.0 copy-done.1
  113.1 0.0 copy-start.2
  113.1 1.0 copy-done.2
  114.1 82.0 %attention.1 = bf16[128,4096]{1,0:T(8,128)(2,1)S(1)} custom-call(bf16[4,512,128]{2,1,0:T(8,128)(2,1)S(1)} %copy-done.1, bf16[2,512,256]{2,1,0:T(8,128)(2,1)S(1)} %copy-done.2, bf16[256,4096]{1,0:T(8,128)(2,1)S(1)} %copy-done, bf16[2,128,4096]{2,1,0:T(8,128)(2,1)} %get-tuple-element.10.wo_half), custom_call_target="tpu_custom_call" | custom-call | tf_op jit(solution)/shard_map/attention/pallas_call | solution.py:665
  196.1 1.0 copy.26
  (6 shorter events, 0.0 us)
Async XLA Ops:
  0.0 7.7 %copy-start.3 = (bf16[128,1,4096]{2,0,1:T(8,128)(2,1)S(1)}, bf16[128,1,4096]{2,0,1:T(8,128)(2,1)}, u32[]{:S(2)}) copy-start(bf16[128,1,4096]{2,0,1:T(8,128)(2,1)} %param.22) | copy-start | bytes 3145732
  9.7 102.3 %copy-start = (bf16[256,4096]{1,0:T(8,128)(2,1)S(1)}, bf16[256,4096]{1,0:T(8,128)(2,1)}, u32[]{:S(2)}) copy-start(bf16[256,4096]{1,0:T(8,128)(2,1)} %wo.3) | copy-start | bytes 6291460
  112.0 1.0 copy-start.1
  113.1 1.0 copy-start.2

commit v4 on v3

--- a/solution.py
+++ b/solution.py
@@ -59,11 +59,11 @@
 
 
 def front_kernel(
-    slot_r, count_r, start_r, v, qkvw, outw, t, vec, trig,
+    slot_r, count_r, start_r, v, qkvw, outw, t_raw, ln_gr, ln_br, outb, qkvb, pbr, gainr, trig,
     proj, wq, wk, wv, wo,
     q_out, kv_out, wo_half,
-    ws, wg, vp, tg, pw, wc, fold, plain, st, nrm, qk, vv, ctx, ctxo, pool, poolo, tok, land, table, col,
-    local, wss, wrs, tss, trs, hss, hrs, vss, vrs, ess, ers, sss, srs, xss, xrs, pss, prs, oss, ors,
+    t, ws, wg, vp, tg, pw, wc, fold, plain, st, nrm, qk, vv, ctx, ctxo, pool, poolo, tok, land, table, col, prow,
+    local, wss, wrs, tss, trs, hss, hrs, vss, vrs, ess, ers, sss, srs, xss, xrs, pss, prs, oss, ors, fxr, fps, fpr,
 ):
     f, s, xs, ys, zs, fp = places()
     core = f % 2
@@ -74,11 +74,17 @@
     def lanes(first):
         return pl.ds(pl.multiple_of(first + core * 640, 128), 640)
 
+    def halved(ref, first):
+        row = ref[...][None]
+        return jnp.where(
+            core == 0, row[:, first : first + 640], row[:, first + 640 : first + 1280]
+        )
+
     def landed(dst, recv):
         remote(dst, dst, vss, recv, fp, s).wait_recv()
 
-    ln_g, ln_b = vec[:, :1280], vec[:, 1280:2560]
-    pb, again = vec[:, 7680:11776], vec[:, 11776:]
+    ln_g, ln_b = ln_gr[...][None], ln_br[...][None]
+    pb, again = pbr[...][None], gainr[...][None]
     packs = [
         pltpu.make_async_copy(qkvw.at[:, lanes(0)], ws.at[0, :, pl.ds(0, 640)], local.at[0]),
         pltpu.make_async_copy(qkvw.at[:, lanes(1280)], ws.at[0, :, pl.ds(640, 640)], local.at[1]),
@@ -91,8 +97,13 @@
         pltpu.make_async_copy(wv, wc.at[:, pl.ds(384, 128)], local.at[6]),
         pltpu.make_async_copy(proj, pw, local.at[7]),
     ]
-    for copy in packs:
+    for copy in packs + loads:
         copy.start()
+    for i in range(4):
+        rows = slice(i * 32, i * 32 + 32)
+        x = t_raw[rows, :].astype(F32)
+        x = x * lax.rsqrt(jnp.mean(x * x, axis=1, keepdims=True) + 1e-5)
+        t[rows, :] = (x * again).astype(BF)
     greet(
         [(f, seq_at(k)) for k in range(1, 16)]
         + [(xs(k), s) for k in (1, 2, 3)]
@@ -115,24 +126,30 @@
     def weight_half(ref, n):
         return ref.at[:, pl.ds(n * 640, 640)]
 
-    def send_weights(j, k):
+    def weight_copy(h, j, k, n, a, b, at, to):
+        go(remote(a, b, wss.at[h, j, k, n], wrs.at[(h,) + at], f, to))
+
+    def start_weights():
+        for h in range(2):
+            first = (ys, zs)[h]
+            slot = weight_slot(h, 0, 0)
+            weight_copy(h, 0, 0, 0, ws.at[h], slot, (1, 0, 0), first(1))
+            weight_copy(h, 0, 0, 1, ws.at[h], slot, (3, 0, 0), first(3))
+
+    def pass_weights(j):
+        for h in range(2):
+            second = (zs, ys)[h]
+            slot = weight_slot(h, j, 0)
+            full = ws.at[h] if j == 0 else slot
+            weight_copy(h, j, 0, 2, full, slot, (j, 1, 0), second(1))
+            weight_copy(h, j, 0, 3, full, slot, (j, 3, 0), second(3))
+
+    def relay_weights(j, k):
         for h in range(2):
             first, second = (ys, zs) if h == 0 else (zs, ys)
-            slot = weight_slot(h, j, k)
-            full = ws.at[h] if j == k == 0 else slot
-            plan = []
-            if j == k == 0:
-                plan += [(full, slot, (1, 0, 0), first(1)), (full, slot, (3, 0, 0), first(3))]
-            if k == 0 and j in (1, 3):
-                part = weight_half(slot, j // 2)
-                plan += [(part, part, (2, 0, j // 2), first(j))]
-            if k == 0:
-                plan += [(full, slot, (j, 1, 0), second(1)), (full, slot, (j, 3, 0), second(3))]
-            if k in (1, 3):
-                part = weight_half(slot, k // 2)
-                plan += [(part, part, (j, 2, k // 2), second(k))]
-            for n, (a, b, (jj, kk, m), to) in enumerate(plan):
-                go(remote(a, b, wss.at[h, j, k, n], wrs.at[h, jj, kk, m], f, to))
+            n, at, to = (j // 2, (2, 0), first(j)) if k == 0 else (k // 2, (j, 2), second(k))
+            part = weight_half(weight_slot(h, j, k), n)
+            weight_copy(h, j, k, 0, part, part, at + (n,), to)
 
     def take_weights(j, k):
         for h in range(2):
@@ -142,15 +159,14 @@
                 landed(weight_half(slot, 1), wrs.at[h, j, k, 1])
             else:
                 landed(slot, wrs.at[h, j, k, 0])
-        send_weights(j, k)
-
-    send_weights(0, 0)
+        if k in (1, 3):
+            relay_weights(j, k)
+
+    start_weights()
     go(remote(v, vp, vss, vrs, fp, s))
     go(remote(t, tg.at[f], tss.at[0], trs.at[1], xs(1), s))
     go(remote(t, tg.at[f], tss.at[1], trs.at[3], xs(3), s))
     go(remote(t, tg.at[f], hss.at[0, 0], hrs.at[0, 0], fp, s))
-    for copy in loads:
-        copy.start()
     wg[0, s] = ws[0]
     wg[1, s] = ws[1]
     slot = slot_r[...]
@@ -198,16 +214,18 @@
     lax.fori_loop(0, 3, fold_rows, 0)
     take_weights(1, 0)
     take_weights(3, 0)
+    relay_weights(1, 0)
+    relay_weights(3, 0)
+    pass_weights(0)
     lax.fori_loop(3, 6, fold_rows, 0)
+    pass_weights(1)
+    lax.fori_loop(6, 8, fold_rows, 0)
+    take_weights(2, 0)
+    pass_weights(2)
+    pass_weights(3)
     take_weights(0, 1)
     take_weights(0, 3)
-    take_weights(2, 0)
-    lax.fori_loop(6, 8, fold_rows, 0)
-    take_weights(1, 1)
-    take_weights(1, 3)
     lax.fori_loop(8, 10, fold_rows, 0)
-    take_weights(3, 1)
-    take_weights(3, 3)
     row = lax.broadcasted_iota(jnp.int32, (16, 1), 0)
     biased = pb * again
     upper = biased.astype(BF).astype(F32)
@@ -218,6 +236,8 @@
     fold[640:768, :] = jnp.where(first, biased, 0.0).astype(BF)
     fold[1408:1536, :] = jnp.zeros((128, 512), BF)
     text_rows(t, f)
+    take_weights(1, 1)
+    take_weights(1, 3)
     landed(vp, vrs)
     for a in range(2):
         pick = facts[a][0]
@@ -236,8 +256,6 @@
         return carry
 
     lax.fori_loop(0, 4, norm_rows, 0)
-    take_weights(2, 1)
-    take_weights(2, 3)
     for j in (1, 3):
         fs = xs(4 - j)
         here = tg.at[fs]
@@ -248,8 +266,12 @@
     for n in range(2):
         half = pl.ds(n * 128, 128)
         go(remote(wo.at[half], wo_half.at[n], oss.at[n], ors.at[n], xs(1 + 2 * n), s))
-    for j in (1, 3):
-        text_rows(tg.at[xs(4 - j)], xs(4 - j))
+    take_weights(2, 1)
+    take_weights(2, 3)
+    text_rows(tg.at[xs(3)], xs(3))
+    take_weights(3, 1)
+    take_weights(3, 3)
+    text_rows(tg.at[xs(1)], xs(1))
     landed(tg.at[fp], hrs.at[0, 0])
     text_rows(tg.at[fp], fp)
     take_weights(0, 2)
@@ -275,10 +297,10 @@
         rows = pl.ds(pl.multiple_of(i * 128, 128), 128)
         n = nrm[rows, :]
         both = jnp.dot(n, wg[0].reshape(1280, 1280), preferred_element_type=F32)
-        qk[rows, :640] = (both[:, :640] + vec[:, lanes(3840)]).astype(BF)
-        qk[rows, 640:] = (both[:, 640:] + vec[:, lanes(5120)]).astype(BF)
+        qk[rows, :640] = (both[:, :640] + halved(qkvb, 0)).astype(BF)
+        qk[rows, 640:] = (both[:, 640:] + halved(qkvb, 1280)).astype(BF)
         third = jnp.dot(n, wg[1, :, :, :640].reshape(1280, 640), preferred_element_type=F32)
-        vv[rows, :] = (third + vec[:, lanes(6400)]).astype(BF)
+        vv[rows, :] = (third + halved(qkvb, 2560)).astype(BF)
         return carry
 
     lax.fori_loop(0, 4, project, 0)
@@ -306,7 +328,7 @@
     attended = jnp.dot(ctx[...], out_rows(core), preferred_element_type=F32)
     landed(ctxo, ers.at[0])
     attended = attended + jnp.dot(ctxo[...], out_rows(1 - core), preferred_element_type=F32)
-    hidden = (st[:, lanes(0)].astype(F32) + attended + vec[:, lanes(2560)]).astype(BF)
+    hidden = (st[:, lanes(0)].astype(F32) + attended + halved(outb, 0)).astype(BF)
     quarter = lax.broadcasted_iota(jnp.int32, (128, 512), 1) // 4 == lax.broadcasted_iota(
         jnp.int32, (128, 512), 0
     )
@@ -323,9 +345,10 @@
         other_rows = pl.ds(pl.multiple_of(640 - core * 640, 128), 640)
         seen = jnp.dot(pool[...], pw[own_rows, cols], preferred_element_type=F32)
         seen = seen + jnp.dot(poolo[...], pw[other_rows, cols], preferred_element_type=F32)
-        seen = seen + vec[:, pl.ds(pl.multiple_of(7680 + c * 512, 128), 512)]
+        seen = seen + prow[:, pl.ds(pl.multiple_of(c * 512, 128), 512)]
         return total + jnp.sum(seen * seen, axis=1, keepdims=True)
 
+    prow[...] = pb
     total = lax.fori_loop(0, 8, square, jnp.zeros((128, 1), F32))
     scale = lax.rsqrt(total * (1.0 / 4096) + 1e-5)
     head = (pool[...].astype(F32) * scale).astype(BF)
@@ -345,16 +368,24 @@
     land[s] = tok[s]
     for k in range(1, 16):
         landed(land.at[seq_at(16 - k)], srs.at[k])
-    for i, k in enumerate(NEAR_FIRST):
-        go(remote(land, table.at[f], xss.at[i], xrs.at[k], xs(k), s))
+    go(remote(land, table.at[f], xss.at[0], xrs.at[1], xs(1), s))
+    go(remote(land, table.at[f], xss.at[1], xrs.at[3], xs(3), s))
     go(remote(land, table.at[f], pss.at[0], prs.at[0], fp, s))
     table[f] = land[...]
-    for j in NEAR_FIRST:
+    for j in (1, 3):
         fs = xs(4 - j)
         landed(table.at[fs], xrs.at[j])
+        part = table.at[fs, pl.ds(j // 2 * 8, 8)]
+        go(remote(part, part, xss.at[2 + j // 2], fxr.at[j // 2], xs(j), s))
         go(remote(table.at[fs], table.at[fs], pss.at[j], prs.at[j], fp, s))
-    for j in range(4):
+    for n in range(2):
+        part = table.at[xs(2), pl.ds(n * 8, 8)]
+        landed(part, fxr.at[n])
+        go(remote(part, part, fps.at[n], fpr.at[n], fp, s))
+    for j in (0, 1, 3):
         landed(table.at[(f // 2 + 4 - j) % 4 * 2 + 1 - core], prs.at[j])
+    for n in range(2):
+        landed(table.at[xs(2) + 1 - 2 * core, pl.ds(n * 8, 8)], fpr.at[n])
     parts = []
     for x in range(4):
         even = table[2 * x].astype(F32).reshape(128, 768).astype(BF)
@@ -412,6 +443,7 @@
         in_specs=[vmem] * (len(rows) + len(vmem_args)) + [hbm] * len(hbm_args),
         out_specs=(vmem, vmem, hbm),
         scratch_shapes=[
+            buf((128, 4096), BF),
             buf((2, 80, 1280), BF),
             buf((2, 16, 80, 1280), BF),
             buf((2, 256, 1280), BF),
@@ -432,6 +464,7 @@
             buf((16, 8, 768), BF),
             buf((8, 16, 8, 768), BF),
             buf((128, 128), jnp.int32),
+            buf((1, 4096), F32),
             dma((8,)),
             dma((2, 4, 4, 4)),
             dma((2, 4, 4, 2)),
@@ -445,10 +478,13 @@
             dma((2,)),
             dma((16,)),
             dma((16,)),
-            dma((3,)),
             dma((4,)),
             dma((4,)),
             dma((4,)),
+            dma((4,)),
+            dma((2,)),
+            dma((2,)),
+            dma((2,)),
             dma((2,)),
             dma((2,)),
         ],
@@ -481,18 +517,27 @@
 
 
 ORDER = (
-    (0, 0), (1, 0), (3, 0), (0, 1), (0, 3), (2, 0), (1, 1), (1, 3),
-    (3, 1), (3, 3), (0, 2), (2, 1), (2, 3), (1, 2), (3, 2), (2, 2),
+    (0, 0), (1, 0), (3, 0), (2, 0), (0, 1), (0, 3), (1, 1), (1, 3),
+    (0, 2), (3, 1), (3, 3), (1, 2), (2, 1), (2, 3), (3, 2), (2, 2),
 )
+TAKEN = {1: ((1, 0), (3, 0)), 2: (), 4: ((0, 1), (0, 3)), 5: ()}
+PASSED = {1: (0,), 3: (1,), 4: (3,), 6: (2,)}
+RELAYED = {1: ((1, 0), (3, 0)), 4: ((0, 1), (0, 3)), 5: ()}
 
 
 def attention_kernel(
-    q, own, wo, wo_half, out, kv, acc, top, den, ctx, seen, lhs, wog, give, got,
+    q_far, own_far, wo, wo_half, out, q, own, kv, acc, top, den, ctx, seen, via, lhs, wog, give, got,
     local, ss, rs, css, crs, oss, ors, gss, grs,
 ):
     f, s, xs, ys, zs, fp = places()
     core = f % 2
     y, z = s // 4, s % 4
+    brought = [
+        pltpu.make_async_copy(own_far, own, local.at[4]),
+        pltpu.make_async_copy(q_far, q, local.at[5]),
+    ]
+    for copy in brought:
+        copy.start()
     greet(
         [(f, ys(1)), (f, ys(3)), (f, zs(1)), (f, zs(3))]
         + [(xs(k), s) for k in (1, 2, 3)]
@@ -508,25 +553,45 @@
     def half_of(ref, n):
         return ref.at[pl.ds(n * 256, 256)]
 
-    def copies_of(j, k):
+    def kv_copy(h, j, k, n, a, b, at, to):
+        return remote(a, b, ss.at[h, j, k, n], rs.at[(h,) + at], f, to)
+
+    def start_copies():
+        result = []
+        for h in range(2):
+            first = (ys, zs)[h]
+            slot = slot_of(h, 0, 0)
+            result.append(kv_copy(h, 0, 0, 0, own.at[h], slot, (1, 0, 0), first(1)))
+            result.append(kv_copy(h, 0, 0, 1, own.at[h], slot, (3, 0, 0), first(3)))
+        return result
+
+    def pass_copies(j):
+        result = []
+        for h in range(2):
+            second = (zs, ys)[h]
+            slot = slot_of(h, j, 0)
+            full = own.at[h] if j == 0 else slot
+            result.append(kv_copy(h, j, 0, 2, full, slot, (j, 1, 0), second(1)))
+            result.append(kv_copy(h, j, 0, 3, full, slot, (j, 3, 0), second(3)))
+        return result
+
+    def relay_copies(j, k):
         result = []
         for h in range(2):
             first, second = (ys, zs) if h == 0 else (zs, ys)
-            slot = slot_of(h, j, k)
-            full = own.at[h] if j == k == 0 else slot
-            plan = []
-            if j == k == 0:
-                plan += [(full, slot, (1, 0, 0), first(1)), (full, slot, (3, 0, 0), first(3))]
-            if k == 0 and j in (1, 3):
-                part = half_of(slot, j // 2)
-                plan += [(part, part, (2, 0, j // 2), first(j))]
-            if k == 0:
-                plan += [(full, slot, (j, 1, 0), second(1)), (full, slot, (j, 3, 0), second(3))]
-            if k in (1, 3):
-                part = half_of(slot, k // 2)
-                plan += [(part, part, (j, 2, k // 2), second(k))]
-            for n, (a, b, (jj, kk, m), to) in enumerate(plan):
-                result.append(remote(a, b, ss.at[h, j, k, n], rs.at[h, jj, kk, m], f, to))
+            n, at, to = (j // 2, (2, 0), first(j)) if k == 0 else (k // 2, (j, 2), second(k))
+            part = half_of(slot_of(h, j, k), n)
+            result.append(kv_copy(h, j, k, 0, part, part, at + (n,), to))
+        return result
+
+    def copies_at(n):
+        j, k = ORDER[n]
+        relayed = RELAYED.get(n, ((j, k),) if k in (1, 3) else ())
+        result = []
+        for jj, kk in relayed:
+            result += relay_copies(jj, kk)
+        for jj in PASSED.get(n, ()):
+            result += pass_copies(jj)
         return result
 
     def landed(dst, recv):
@@ -541,7 +606,9 @@
             else:
                 landed(slot, rs.at[h, j, k, 0])
 
-    for copy in copies_of(0, 0):
+    for copy in brought:
+        copy.wait()
+    for copy in start_copies():
         copy.start()
     lower, upper = pl.ds(0, 128), pl.ds(128, 128)
     parts = [
@@ -571,9 +638,10 @@
                 k = jnp.where(i == n, kk, k)
 
                 @pl.when(i == n)
-                def _(jj=jj, kk=kk):
-                    take(jj, kk)
-                    for copy in copies_of(jj, kk):
+                def _(n=n, jj=jj, kk=kk):
+                    for at in TAKEN.get(n, ((jj, kk),)):
+                        take(*at)
+                    for copy in copies_at(n):
                         copy.start()
 
         a = (y + 4 - j) % 4 * 4 + (z + 4 - k) % 4
@@ -596,22 +664,35 @@
             for owner in range(8):
                 start = head * 256 + owner * 32
                 ctx[owner // 2, owner % 2, tile, head] = block[start : start + 32]
-    for j, k in ORDER:
-        for copy in copies_of(j, k):
+    for copy in start_copies():
+        copy.wait_send()
+    for n in range(1, 16):
+        for copy in copies_at(n):
             copy.wait_send()
     x = f // 2
-    last = []
-    for i, k in enumerate(NEAR_FIRST):
-        last.append(remote(ctx.at[(x + k) % 4], seen.at[4 - k], css.at[i], crs.at[k], xs(k), s))
-    for copy in last:
+    far = (x + 2) % 4
+    last = [
+        remote(ctx.at[far, 0], via.at[0], css.at[0], crs.at[0], xs(1), s),
+        remote(ctx.at[far, 1], via.at[1], css.at[1], crs.at[1], xs(3), s),
+        remote(ctx.at[(x + 1) % 4], seen.at[3], css.at[2], crs.at[2], xs(1), s),
+        remote(ctx.at[(x + 3) % 4], seen.at[1], css.at[3], crs.at[3], xs(3), s),
+        remote(via.at[0], seen.at[2, 0], css.at[4], crs.at[4], xs(1), s),
+        remote(via.at[1], seen.at[2, 1], css.at[5], crs.at[5], xs(3), s),
+    ]
+    for copy in last[:4]:
         copy.start()
     seen[0] = ctx[x]
+    for n in range(2):
+        landed(via.at[n], crs.at[n])
+        last[4 + n].start()
     for copy in keeps:
         copy.wait()
     for copy in parts:
         copy.wait()
-    for k in (1, 3, 2):
-        landed(seen.at[4 - k], crs.at[k])
+    landed(seen.at[3], crs.at[2])
+    landed(seen.at[1], crs.at[3])
+    landed(seen.at[2, 0], crs.at[4])
+    landed(seen.at[2, 1], crs.at[5])
     for d in range(4):
         for head in range(2):
             cols = slice(d * 256 + head * 128, d * 256 + head * 128 + 128)
@@ -665,24 +746,27 @@
     return pl.pallas_call(
         attention_kernel,
         out_shape=jax.ShapeDtypeStruct((128, 4096), BF),
-        in_specs=[vmem, vmem, hbm, hbm],
+        in_specs=[hbm] * 4,
         out_specs=vmem,
         scratch_shapes=[
+            pltpu.VMEM((4, 512, 128), BF),
+            pltpu.VMEM((2, 512, 256), BF),
             pltpu.VMEM((2, 16, 512, 256), BF),
             state,
             state,
             state,
             pltpu.VMEM((4, 2, 4, 2, 32, 128), BF),
             pltpu.VMEM((4, 2, 4, 2, 32, 128), BF),
+            pltpu.VMEM((2, 4, 2, 32, 128), BF),
             pltpu.VMEM((2, 128, 1024), BF),
             pltpu.VMEM((4, 256, 4096), BF),
             pltpu.VMEM((128, 4096), BF),
             pltpu.VMEM((128, 4096), BF),
-            dma((4,)),
+            dma((6,)),
             dma((2, 4, 4, 4)),
             dma((2, 4, 4, 2)),
-            dma((3,)),
-            dma((4,)),
+            dma((6,)),
+            dma((6,)),
             dma((4,)),
             dma((4,)),
             dma((8,)),
@@ -716,19 +800,26 @@
     wo,
 ):
     s = lax.axis_index("seq")
-    text = text_embed.reshape(128, 4096).astype(F32)
-    text = (
-        text * lax.rsqrt(jnp.mean(text * text, axis=1, keepdims=True) + 1e-5) * attn_gain
-    ).astype(BF)
     exponents = jnp.arange(0, 128, 2).astype(F32) / 128
     inverse = jnp.power(F32(ROPE_THETA), -exponents)
     steps = jnp.concatenate([jnp.arange(128) * 128, jnp.arange(8) * 16 + s]).astype(F32)
     angles = steps[:, None] * jnp.concatenate([inverse, inverse])[None, :]
     trig = jnp.stack([jnp.cos(angles), jnp.sin(angles)])
-    vectors = [vit_ln_gain, vit_ln_bias, vit_out_b, vit_qkv_b, proj_b, attn_gain]
     queries, own, wo_half = front(
         [frame_slot[None], patch_count[None], vis_start[None]],
-        [vit_states, vit_qkv_w, vit_out_w, text, jnp.concatenate(vectors)[None], trig],
+        [
+            vit_states,
+            vit_qkv_w,
+            vit_out_w,
+            text_embed.reshape(128, 4096),
+            vit_ln_gain,
+            vit_ln_bias,
+            vit_out_b,
+            vit_qkv_b,
+            proj_b,
+            attn_gain,
+            trig,
+        ],
         [proj_w, wq, wk, wv, wo],
     )
     return attention(queries, own, wo, wo_half).reshape(128, 1, 4096)

time: 198 us -> 174 us (0.88)
  Pallas kernels: 184 us -> 169 us
  local copies, waits for them, and re-layouts: 8.01 us -> 3.05 us
  other arithmetic: 4.71 us -> 1.1 us
    pallas_call x1, Pallas kernels: 102 us -> 94.7 us  [front(): pl.pallas_call(front_kernel, out_shape=(shape((4, 512, 128), BF), shape((...]
    pallas_call x1, Pallas kernels: 82 us -> 74.6 us  [attention(): pl.pallas_call(attention_kernel, out_shape=jax.ShapeDtypeStruct((128, 409...]
    unnamed x14 -> x7, local copies, waits for them, and re-layouts: 6.62 us -> 3.05 us
    convert_element_type x1 -> x0, other arithmetic: 2.01 us -> none  [per_device(): text = (text * lax.rsqrt(jnp.mean(text * text, axis=1, keepdims=True) + 1...]
where the time goes in v4:
time: 174 us; the launch traced here: 173 us
  Pallas kernels  169 us (97%)
  local copies, waits for them, and re-layouts  3.05 us (2%)
    pallas_call x1, Pallas kernels, front(): pl.pallas_call(front_kernel, out_shape=(shape((4, 512, 128), BF), shape((...  94.7 us
    pallas_call x1, Pallas kernels, attention(): pl.pallas_call(attention_kernel, out_shape=jax.ShapeDtypeStruct((128, 409...  74.6 us

profile of v4, /device:TPU:1, one launch (start us, length us, event | category | flops | bytes accessed | tf_op | source)
XLA Modules:
  0.0 173.5 jit_solution(5660066160192092843)
XLA Ops:
  0.0 0.1 pad_maximum_fusion.1
  0.1 0.3 multiply_cosine_fusion
  0.4 0.7 pad_maximum_fusion.trig
  1.1 0.0 copy-start
  1.1 94.7 %front.1 = (bf16[4,512,128]{2,1,0:T(8,128)(2,1)}, bf16[2,512,256]{2,1,0:T(8,128)(2,1)}, bf16[2,128,4096]{2,1,0:T(8,128)(2,1)}) custom-call(s32[1,128]{1,0:T(1,128)} %bitcast.7, s32[1,128]{1,0:T(1,128)} %bitcast.8, s32[1,128]{1,0:T(1,128)} %bitcast.9, bf16[2,256,1280]{2,1,0:T(8,128)(2,1)} %v.1, bf16[80,3840]{1,0:T(8,128)(2,1)} %qkvw.1, ...), custom_call_target="tpu_custom_call" | custom-call | tf_op jit(solution)/shard_map/front/pallas_call | solution.py:436
  95.9 0.0 copy-done
  95.9 0.0 copy-start.1
  95.9 1.0 copy-done.1
  96.9 0.0 copy-start.2
  96.9 1.0 copy-done.2
  98.0 74.6 %attention.1 = bf16[128,4096]{1,0:T(8,128)(2,1)S(1)} custom-call(bf16[4,512,128]{2,1,0:T(8,128)(2,1)S(1)} %copy-done.1, bf16[2,512,256]{2,1,0:T(8,128)(2,1)S(1)} %copy-done.2, bf16[256,4096]{1,0:T(8,128)(2,1)S(1)} %copy-done, bf16[2,128,4096]{2,1,0:T(8,128)(2,1)} %get-tuple-element.10.wo_half), custom_call_target="tpu_custom_call" | custom-call | tf_op jit(solution)/shard_map/attention/pallas_call | solution.py:746
  172.5 1.0 copy.20
  (4 shorter events, 0.0 us)
Async XLA Ops:
  1.1 94.7 %copy-start = (bf16[256,4096]{1,0:T(8,128)(2,1)S(1)}, bf16[256,4096]{1,0:T(8,128)(2,1)}, u32[]{:S(2)}) copy-start(bf16[256,4096]{1,0:T(8,128)(2,1)} %wo.3) | copy-start | bytes 6291460
  95.9 1.0 copy-start.1
  96.9 1.0 copy-start.2

commit v5 on v4

--- a/solution.py
+++ b/solution.py
@@ -313,10 +313,10 @@
             val = vv[rows, h * 80 : h * 80 + 80]
             scores = lax.dot_general(
                 q, k, (((1,), (1,)), ((), ())), preferred_element_type=F32
-            ) * (1.0 / math.sqrt(80))
+            ) * (math.log2(math.e) / math.sqrt(80))
             scores = jnp.where(live, scores, NEG)
-            weights = jnp.exp(scores - jnp.max(scores, axis=1, keepdims=True))
-            prob = (weights / jnp.sum(weights, axis=1, keepdims=True)).astype(BF)
+            weights = jnp.exp2(scores - jnp.max(scores, axis=1, keepdims=True))
+            prob = (weights * (1.0 / jnp.sum(weights, axis=1, keepdims=True))).astype(BF)
             ctx[rows, h * 80 : h * 80 + 80] = jnp.dot(
                 prob, val, preferred_element_type=F32
             ).astype(BF)
@@ -773,7 +773,7 @@
             dma((8,)),
         ],
         compiler_params=pltpu.CompilerParams(
-            collective_id=3, has_side_effects=True, vmem_limit_bytes=48 << 20
+            collective_id=3, has_side_effects=True, vmem_limit_bytes=63 << 20
         ),
         name="attention",
     )(q, own, wo, wo_half)

time: 174 us -> 174 us (level)
  no operation moved by 1% of the time
where the time goes in v5:
time: 174 us; the launch traced here: 173 us
  Pallas kernels  170 us (98%)
  local copies, waits for them, and re-layouts  2.29 us (1%)
    pallas_call x1, Pallas kernels, front(): pl.pallas_call(front_kernel, out_shape=(shape((4, 512, 128), BF), shape((...  94.5 us
    pallas_call x1, Pallas kernels, attention(): pl.pallas_call(attention_kernel, out_shape=jax.ShapeDtypeStruct((128, 409...  75.5 us

profile of v5, /device:TPU:1, one launch (start us, length us, event | category | flops | bytes accessed | tf_op | source)
XLA Modules:
  0.0 173.5 jit_solution(12405571755112588252)
XLA Ops:
  0.0 0.1 pad_maximum_fusion.1
  0.1 0.3 multiply_cosine_fusion
  0.4 0.7 pad_maximum_fusion.trig
  1.1 94.5 %front.1 = (bf16[4,512,128]{2,1,0:T(8,128)(2,1)}, bf16[2,512,256]{2,1,0:T(8,128)(2,1)}, bf16[2,128,4096]{2,1,0:T(8,128)(2,1)}) custom-call(s32[1,128]{1,0:T(1,128)} %bitcast.7, s32[1,128]{1,0:T(1,128)} %bitcast.8, s32[1,128]{1,0:T(1,128)} %bitcast.9, bf16[2,256,1280]{2,1,0:T(8,128)(2,1)} %v.1, bf16[80,3840]{1,0:T(8,128)(2,1)} %qkvw.1, ...), custom_call_target="tpu_custom_call" | custom-call | tf_op jit(solution)/shard_map/front/pallas_call | solution.py:436
  95.6 75.5 %attention.1 = bf16[128,4096]{1,0:T(8,128)(2,1)} custom-call(bf16[4,512,128]{2,1,0:T(8,128)(2,1)} %get-tuple-element.8.q_far, bf16[2,512,256]{2,1,0:T(8,128)(2,1)} %get-tuple-element.9.own_far, bf16[256,4096]{1,0:T(8,128)(2,1)} %wo.3, bf16[2,128,4096]{2,1,0:T(8,128)(2,1)} %get-tuple-element.10.wo_half), custom_call_target="tpu_custom_call" | custom-call | tf_op jit(solution)/shard_map/attention/pallas_call | solution.py:746
  171.2 2.3 %copy.20 = bf16[128,1,4096]{2,0,1:T(8,128)(2,1)} copy(bf16[128,1,4096]{2,0,1:T(8,128)(2,1)} %bitcast.5) | data formatting | bytes 2097152
  (4 shorter events, 0.0 us)
